TPU v7x, 32 devices: a whole 2x2x4 slice. The times are simulated.
32 devices in a mesh: south: 2 (over core), east: 4 (over z), down: 2 (over x), ens: 2 (over y).
Axes of the slice: x: 2, y: 2, z: 4, core: 2. Of those that a mesh axis runs over, the one named last changes fastest.
Arguments:
- density: float32 [16, 128, 128, 128], P(('ens', 'south'), 'east', 'down'), parts along dimension 0, may hold values from 0.2 to 1.8
- flow_j: float32 [16, 128, 128, 128], P(('ens', 'south'), 'east', 'down'), parts along dimension 0, may hold values from -0.3 to 0.3
- flow_i: float32 [16, 128, 128, 128], P(('ens', 'south'), 'east', 'down'), parts along dimension 0, may hold values from -0.3 to 0.3
- flow_k: float32 [16, 128, 128, 128], P(('ens', 'south'), 'east', 'down'), parts along dimension 0, may hold values from -0.3 to 0.3
Outputs:
- density_end: float32 [16, 128, 128, 128], P(('ens', 'south'), 'east', 'down'), parts along dimension 0
There are 2 independent parts, one for each index of `ens`. A program takes and returns all parts, laid end to end along the dimension named above; each array names one. Nothing has to cross between parts.
All inputs are finite; a program needn't handle non-finite values.
Results may differ from a plain program's by a relative error of at most 0.00002.
Values sent between devices are 32-bit elements; how exact they have to be, the bound alone decides.
No kernel may reach another device: no remote copies, remote signals or barrier semaphores. Data moves between devices by JAX's collectives and lax.ppermute only.
A program may use at most 192 MiB of HBM per device.

v0:
```python
import jax
import jax.numpy as jnp
from jax import lax
from jax.sharding import PartitionSpec as P

STEPS = 3


def padded_2(x, sides, width):
    for axis, dim in sides:
        count, length = (lax.axis_size(axis), x.shape[dim])
        up = [(i, (i + 1) % count) for i in range(count - 1)]
        down = [(j, i) for i, j in up]
        last = lax.slice_in_dim(x, length - width, length, axis=dim)
        initial = lax.slice_in_dim(x, 0, width, axis=dim)
        before = lax.ppermute(last, axis, up)
        after = lax.ppermute(initial, axis, down)
        x = jnp.concatenate([before, x, after], axis=dim)
    return x


def inner_cells(values, dims):
    for dim in dims:
        values = lax.slice_in_dim(values, 1, values.shape[dim] - 1, axis=dim)
    return values


def side_cells(values, dim, start, dims):
    others = [other for other in dims if other != dim]
    values = inner_cells(values, others)
    return lax.slice_in_dim(values, start, start + values.shape[dim] - 2, axis=dim)


def advance(padded, flow_j, flow_i, flow_k):
    middle = inner_cells(padded, (0, 1, 2))
    lower = [side_cells(padded, dim, 0, (0, 1, 2)) for dim in (0, 1, 2)]
    upper = [side_cells(padded, dim, 2, (0, 1, 2)) for dim in (0, 1, 2)]
    slopes = [above - below for above, below in zip(upper, lower)]
    smooth_rate = 0.05
    spread = lower[0] + upper[0] + lower[1] + upper[1] + lower[2] + upper[2] - 6.0 * middle
    return (
        middle - flow_j * slopes[0] - flow_i * slopes[1] - flow_k * slopes[2] + smooth_rate * spread
    )


def per_device(density, flow_j, flow_i, flow_k):
    for step in range(STEPS):
        padded = padded_2(density, (("south", 0), ("east", 1), ("down", 2)), 1)
        density = advance(padded, flow_j, flow_i, flow_k)
    return density


def solution(mesh):
    in_specs = (
        P(("ens", "south"), "east", "down", None),
        P(("ens", "south"), "east", "down", None),
        P(("ens", "south"), "east", "down", None),
        P(("ens", "south"), "east", "down", None),
    )
    out_specs = P(("ens", "south"), "east", "down", None)
    return jax.shard_map(
        per_device, mesh=mesh, in_specs=in_specs, out_specs=out_specs, check_vma=False
    )
```

profile of v0, /device:TPU:0, one launch (start us, length us, event | category | flops | bytes accessed | tf_op | source)
XLA Modules:
  0.0 118.4 jit_solution(15454010434939045153)
XLA Ops:
  0.0 1.8 %fusion.3 = (f32[1,32,64,128]{3,2,1,0:T(8,128)S(1)}, f32[1,32,64,128]{3,2,1,0:T(8,128)S(1)}) fusion(f32[4,32,64,128]{3,2,1,0:T(8,128)} %param.4), kind=kLoop, calls=%fused_computation.74 | loop fusion | bytes 4194304 | tf_op jit(solution)/shard_map/slice | solution.py:15
  1.8 2.6 %collective-permute-start.1 = (f32[1,32,64,128]{3,2,1,0:T(8,128)S(1)}, f32[1,32,64,128]{3,2,1,0:T(8,128)S(1)}, u32[]{:S(2)}, u32[]{:S(2)}) collective-permute-start(f32[1,32,64,128]{3,2,1,0:T(8,128)S(1)} %get-tuple-element.22), channel_id=1, source_target_pairs={{0,16},{1,17},{2,18},{3,19},{4,20},{5,21},{6,22},{7,23},{8,24},{9,... | collective-permute-start | bytes 3145736 | tf_op jit(solution)/shard_map/ppermute | solution.py:16
  4.4 1.3 %collective-permute-start = (f32[1,32,64,128]{3,2,1,0:T(8,128)S(1)}, f32[1,32,64,128]{3,2,1,0:T(8,128)S(1)}, u32[]{:S(2)}, u32[]{:S(2)}) collective-permute-start(f32[1,32,64,128]{3,2,1,0:T(8,128)S(1)} %get-tuple-element.21), channel_id=1, source_target_pairs={{16,0},{17,1},{18,2},{19,3},{20,4},{21,5},{22,6},{23,7},{24,8},{25... | collective-permute-start | bytes 3145736 | tf_op jit(solution)/shard_map/ppermute | solution.py:17
  7.3 1.7 %collective-permute-done = f32[1,32,64,128]{3,2,1,0:T(8,128)S(1)} collective-permute-done((f32[1,32,64,128]{3,2,1,0:T(8,128)S(1)}, f32[1,32,64,128]{3,2,1,0:T(8,128)S(1)}, u32[]{:S(2)}, u32[]{:S(2)}) %collective-permute-start) | collective-permute-done | bytes 1048608 | tf_op jit(solution)/shard_map/ppermute | solution.py:17
  9.1 4.3 %collective-permute-start.3 = (f32[6,1,64,128]{3,2,1,0:T(8,128)S(1)}, f32[6,1,64,128]{3,2,1,0:T(8,128)S(1)}, u32[]{:S(2)}, u32[]{:S(2)}) collective-permute-start(f32[6,1,64,128]{3,2,1,0:T(8,128)S(1)} %get-tuple-element.15), channel_id=1, source_target_pairs={{0,4},{4,8},{8,12},{1,5},{5,9},{9,13},{2,6},{6,10},{10,14},{3,7},{... | collective-permute-start | bytes 589832 | tf_op jit(solution)/shard_map/ppermute | solution.py:16
  13.4 1.3 %collective-permute-start.2 = (f32[6,1,64,128]{3,2,1,0:T(8,128)S(1)}, f32[6,1,64,128]{3,2,1,0:T(8,128)S(1)}, u32[]{:S(2)}, u32[]{:S(2)}) collective-permute-start(f32[6,1,64,128]{3,2,1,0:T(8,128)S(1)} %get-tuple-element.16), channel_id=1, source_target_pairs={{4,0},{8,4},{12,8},{5,1},{9,5},{13,9},{6,2},{10,6},{14,10},{7,3},{... | collective-permute-start | bytes 589832 | tf_op jit(solution)/shard_map/ppermute | solution.py:17
  14.7 3.1 %collective-permute-done.3 = f32[6,1,64,128]{3,2,1,0:T(8,128)S(1)} collective-permute-done((f32[6,1,64,128]{3,2,1,0:T(8,128)S(1)}, f32[6,1,64,128]{3,2,1,0:T(8,128)S(1)}, u32[]{:S(2)}, u32[]{:S(2)}) %collective-permute-start.3) | collective-permute-done | bytes 196640 | tf_op jit(solution)/shard_map/ppermute | solution.py:16
  17.9 4.1 %collective-permute-done.2 = f32[6,1,64,128]{3,2,1,0:T(8,128)S(1)} collective-permute-done((f32[6,1,64,128]{3,2,1,0:T(8,128)S(1)}, f32[6,1,64,128]{3,2,1,0:T(8,128)S(1)}, u32[]{:S(2)}, u32[]{:S(2)}) %collective-permute-start.2) | collective-permute-done | bytes 196640 | tf_op jit(solution)/shard_map/ppermute | solution.py:17
  22.2 1.3 %collective-permute-start.4 = (f32[6,34,1,128]{3,1,2,0:T(8,128)S(1)}, f32[6,34,1,128]{3,1,2,0:T(8,128)S(1)}, u32[]{:S(2)}, u32[]{:S(2)}) collective-permute-start(f32[6,34,1,128]{3,1,2,0:T(8,128)S(1)} %copy.22), channel_id=1, source_target_pairs={{2,0},{3,1},{6,4},{7,5},{10,8},{11,9},{14,12},{15,13},{18,16},{19,... | collective-permute-start | bytes 313352 | tf_op jit(solution)/shard_map/ppermute | solution.py:17
  23.5 4.6 %collective-permute-start.5 = (f32[6,34,1,128]{3,1,2,0:T(8,128)S(1)}, f32[6,34,1,128]{3,1,2,0:T(8,128)S(1)}, u32[]{:S(2)}, u32[]{:S(2)}) collective-permute-start(f32[6,34,1,128]{3,1,2,0:T(8,128)S(1)} %copy.24), channel_id=1, source_target_pairs={{0,2},{1,3},{4,6},{5,7},{8,10},{9,11},{12,14},{13,15},{16,18},{17,... | collective-permute-start | bytes 313352 | tf_op jit(solution)/shard_map/ppermute | solution.py:16
  31.2 16.5 %multiply_add_fusion.2 = f32[4,32,64,128]{3,2,1,0:T(8,128)S(1)} fusion(f32[4,32,64,128]{3,2,1,0:T(8,128)} %param.4, f32[4,32,64,128]{3,2,1,0:T(8,128)} %param.7, f32[6,34,1,128]{3,2,1,0:T(1,128)} %copy.23, f32[6,1,64,128]{3,2,1,0:T(8,128)S(1)} %collective-permute-done.2, f32[6,32,64,128]{3,2,1,0:T(8,128)} %copy-done.3, ...), kind=kLoop, calls=%fused_computation.48 | loop fusion | flops 29360128 | bytes 29962240 | tf_op jit(solution)/shard_map/add | solution.py:42
  47.9 1.4 %collective-permute-start.7 = (f32[1,32,64,128]{3,2,1,0:T(8,128)S(1)}, f32[1,32,64,128]{3,2,1,0:T(8,128)S(1)}, u32[]{:S(2)}, u32[]{:S(2)}) collective-permute-start(f32[1,32,64,128]{3,2,1,0:T(8,128)S(1)} %get-tuple-element.19), channel_id=1, source_target_pairs={{0,16},{1,17},{2,18},{3,19},{4,20},{5,21},{6,22},{7,23},{8,24},{9,... | collective-permute-start | bytes 3145736 | tf_op jit(solution)/shard_map/ppermute | solution.py:16
  49.3 1.3 %collective-permute-start.6 = (f32[1,32,64,128]{3,2,1,0:T(8,128)S(1)}, f32[1,32,64,128]{3,2,1,0:T(8,128)S(1)}, u32[]{:S(2)}, u32[]{:S(2)}) collective-permute-start(f32[1,32,64,128]{3,2,1,0:T(8,128)S(1)} %get-tuple-element.20), channel_id=1, source_target_pairs={{16,0},{17,1},{18,2},{19,3},{20,4},{21,5},{22,6},{23,7},{24,8},{25... | collective-permute-start | bytes 3145736 | tf_op jit(solution)/shard_map/ppermute | solution.py:17
  51.5 2.4 %collective-permute-done.6 = f32[1,32,64,128]{3,2,1,0:T(8,128)S(1)} collective-permute-done((f32[1,32,64,128]{3,2,1,0:T(8,128)S(1)}, f32[1,32,64,128]{3,2,1,0:T(8,128)S(1)}, u32[]{:S(2)}, u32[]{:S(2)}) %collective-permute-start.6) | collective-permute-done | bytes 1048608 | tf_op jit(solution)/shard_map/ppermute | solution.py:17
  53.9 3.9 %collective-permute-start.9 = (f32[6,1,64,128]{3,2,1,0:T(8,128)S(1)}, f32[6,1,64,128]{3,2,1,0:T(8,128)S(1)}, u32[]{:S(2)}, u32[]{:S(2)}) collective-permute-start(f32[6,1,64,128]{3,2,1,0:T(8,128)S(1)} %get-tuple-element.13), channel_id=1, source_target_pairs={{0,4},{4,8},{8,12},{1,5},{5,9},{9,13},{2,6},{6,10},{10,14},{3,7},{... | collective-permute-start | bytes 589832 | tf_op jit(solution)/shard_map/ppermute | solution.py:16
  57.8 1.3 %collective-permute-start.8 = (f32[6,1,64,128]{3,2,1,0:T(8,128)S(1)}, f32[6,1,64,128]{3,2,1,0:T(8,128)S(1)}, u32[]{:S(2)}, u32[]{:S(2)}) collective-permute-start(f32[6,1,64,128]{3,2,1,0:T(8,128)S(1)} %get-tuple-element.14), channel_id=1, source_target_pairs={{4,0},{8,4},{12,8},{5,1},{9,5},{13,9},{6,2},{10,6},{14,10},{7,3},{... | collective-permute-start | bytes 589832 | tf_op jit(solution)/shard_map/ppermute | solution.py:17
  59.1 3.1 %collective-permute-done.9 = f32[6,1,64,128]{3,2,1,0:T(8,128)S(1)} collective-permute-done((f32[6,1,64,128]{3,2,1,0:T(8,128)S(1)}, f32[6,1,64,128]{3,2,1,0:T(8,128)S(1)}, u32[]{:S(2)}, u32[]{:S(2)}) %collective-permute-start.9) | collective-permute-done | bytes 196640 | tf_op jit(solution)/shard_map/ppermute | solution.py:16
  62.2 4.1 %collective-permute-done.8 = f32[6,1,64,128]{3,2,1,0:T(8,128)S(1)} collective-permute-done((f32[6,1,64,128]{3,2,1,0:T(8,128)S(1)}, f32[6,1,64,128]{3,2,1,0:T(8,128)S(1)}, u32[]{:S(2)}, u32[]{:S(2)}) %collective-permute-start.8) | collective-permute-done | bytes 196640 | tf_op jit(solution)/shard_map/ppermute | solution.py:17
  66.5 1.3 %collective-permute-start.10 = (f32[6,34,1,128]{3,1,2,0:T(8,128)S(1)}, f32[6,34,1,128]{3,1,2,0:T(8,128)S(1)}, u32[]{:S(2)}, u32[]{:S(2)}) collective-permute-start(f32[6,34,1,128]{3,1,2,0:T(8,128)S(1)} %copy.26), channel_id=1, source_target_pairs={{2,0},{3,1},{6,4},{7,5},{10,8},{11,9},{14,12},{15,13},{18,16},{19,... | collective-permute-start | bytes 313352 | tf_op jit(solution)/shard_map/ppermute | solution.py:17
  67.8 4.6 %collective-permute-start.11 = (f32[6,34,1,128]{3,1,2,0:T(8,128)S(1)}, f32[6,34,1,128]{3,1,2,0:T(8,128)S(1)}, u32[]{:S(2)}, u32[]{:S(2)}) collective-permute-start(f32[6,34,1,128]{3,1,2,0:T(8,128)S(1)} %copy.28), channel_id=1, source_target_pairs={{0,2},{1,3},{4,6},{5,7},{8,10},{9,11},{12,14},{13,15},{16,18},{17,... | collective-permute-start | bytes 313352 | tf_op jit(solution)/shard_map/ppermute | solution.py:16
  73.4 1.4 %collective-permute-done.11 = f32[6,34,1,128]{3,1,2,0:T(8,128)S(1)} collective-permute-done((f32[6,34,1,128]{3,1,2,0:T(8,128)S(1)}, f32[6,34,1,128]{3,1,2,0:T(8,128)S(1)}, u32[]{:S(2)}, u32[]{:S(2)}) %collective-permute-start.11) | collective-permute-done | bytes 104480 | tf_op jit(solution)/shard_map/ppermute | solution.py:16
  74.9 8.0 %multiply_add_fusion.1 = f32[4,32,64,128]{3,2,1,0:T(8,128)S(1)} fusion(f32[4,32,64,128]{3,2,1,0:T(8,128)S(1)} %multiply_add_fusion.2, f32[4,32,64,128]{3,2,1,0:T(8,128)S(1)} %copy-done, f32[6,34,1,128]{3,2,1,0:T(1,128)S(1)} %copy.27, f32[6,1,64,128]{3,2,1,0:T(8,128)S(1)} %collective-permute-done.8, f32[1,32,64,128]{3,2,1,0:T(8,128)S(1)} %collective-permute-done.6, ...), kind=kLoop, calls=%fused_computation.47 | loop fusion | flops 37748736 | bytes 23670784 | tf_op jit(solution)/shard_map/add | solution.py:42
  83.1 1.4 %collective-permute-start.13 = (f32[1,32,64,128]{3,2,1,0:T(8,128)S(1)}, f32[1,32,64,128]{3,2,1,0:T(8,128)S(1)}, u32[]{:S(2)}, u32[]{:S(2)}) collective-permute-start(f32[1,32,64,128]{3,2,1,0:T(8,128)S(1)} %get-tuple-element.17), channel_id=1, source_target_pairs={{0,16},{1,17},{2,18},{3,19},{4,20},{5,21},{6,22},{7,23},{8,24},{9,... | collective-permute-start | bytes 3145736 | tf_op jit(solution)/shard_map/ppermute | solution.py:16
  84.5 1.3 %collective-permute-start.12 = (f32[1,32,64,128]{3,2,1,0:T(8,128)S(1)}, f32[1,32,64,128]{3,2,1,0:T(8,128)S(1)}, u32[]{:S(2)}, u32[]{:S(2)}) collective-permute-start(f32[1,32,64,128]{3,2,1,0:T(8,128)S(1)} %get-tuple-element.18), channel_id=1, source_target_pairs={{16,0},{17,1},{18,2},{19,3},{20,4},{21,5},{22,6},{23,7},{24,8},{25... | collective-permute-start | bytes 3145736 | tf_op jit(solution)/shard_map/ppermute | solution.py:17
  86.7 2.4 %collective-permute-done.12 = f32[1,32,64,128]{3,2,1,0:T(8,128)S(1)} collective-permute-done((f32[1,32,64,128]{3,2,1,0:T(8,128)S(1)}, f32[1,32,64,128]{3,2,1,0:T(8,128)S(1)}, u32[]{:S(2)}, u32[]{:S(2)}) %collective-permute-start.12) | collective-permute-done | bytes 1048608 | tf_op jit(solution)/shard_map/ppermute | solution.py:17
  89.1 3.5 %collective-permute-start.15 = (f32[6,1,64,128]{3,2,1,0:T(8,128)S(1)}, f32[6,1,64,128]{3,2,1,0:T(8,128)S(1)}, u32[]{:S(2)}, u32[]{:S(2)}) collective-permute-start(f32[6,1,64,128]{3,2,1,0:T(8,128)S(1)} %get-tuple-element.11), channel_id=1, source_target_pairs={{0,4},{4,8},{8,12},{1,5},{5,9},{9,13},{2,6},{6,10},{10,14},{3,7},{... | collective-permute-start | bytes 589832 | tf_op jit(solution)/shard_map/ppermute | solution.py:16
  92.6 1.3 %collective-permute-start.14 = (f32[6,1,64,128]{3,2,1,0:T(8,128)S(1)}, f32[6,1,64,128]{3,2,1,0:T(8,128)S(1)}, u32[]{:S(2)}, u32[]{:S(2)}) collective-permute-start(f32[6,1,64,128]{3,2,1,0:T(8,128)S(1)} %get-tuple-element.12), channel_id=1, source_target_pairs={{4,0},{8,4},{12,8},{5,1},{9,5},{13,9},{6,2},{10,6},{14,10},{7,3},{... | collective-permute-start | bytes 589832 | tf_op jit(solution)/shard_map/ppermute | solution.py:17
  93.9 3.1 %collective-permute-done.15 = f32[6,1,64,128]{3,2,1,0:T(8,128)S(1)} collective-permute-done((f32[6,1,64,128]{3,2,1,0:T(8,128)S(1)}, f32[6,1,64,128]{3,2,1,0:T(8,128)S(1)}, u32[]{:S(2)}, u32[]{:S(2)}) %collective-permute-start.15) | collective-permute-done | bytes 196640 | tf_op jit(solution)/shard_map/ppermute | solution.py:16
  97.0 4.1 %collective-permute-done.14 = f32[6,1,64,128]{3,2,1,0:T(8,128)S(1)} collective-permute-done((f32[6,1,64,128]{3,2,1,0:T(8,128)S(1)}, f32[6,1,64,128]{3,2,1,0:T(8,128)S(1)}, u32[]{:S(2)}, u32[]{:S(2)}) %collective-permute-start.14) | collective-permute-done | bytes 196640 | tf_op jit(solution)/shard_map/ppermute | solution.py:17
  102.6 4.6 %collective-permute-start.17 = (f32[6,34,1,128]{3,1,2,0:T(8,128)S(1)}, f32[6,34,1,128]{3,1,2,0:T(8,128)S(1)}, u32[]{:S(2)}, u32[]{:S(2)}) collective-permute-start(f32[6,34,1,128]{3,1,2,0:T(8,128)S(1)} %copy.32), channel_id=1, source_target_pairs={{0,2},{1,3},{4,6},{5,7},{8,10},{9,11},{12,14},{13,15},{16,18},{17,... | collective-permute-start | bytes 313352 | tf_op jit(solution)/shard_map/ppermute | solution.py:16
  108.2 1.4 %collective-permute-done.17 = f32[6,34,1,128]{3,1,2,0:T(8,128)S(1)} collective-permute-done((f32[6,34,1,128]{3,1,2,0:T(8,128)S(1)}, f32[6,34,1,128]{3,1,2,0:T(8,128)S(1)}, u32[]{:S(2)}, u32[]{:S(2)}) %collective-permute-start.17) | collective-permute-done | bytes 104480 | tf_op jit(solution)/shard_map/ppermute | solution.py:16
  109.7 8.7 %multiply_add_fusion = f32[4,32,64,128]{3,2,1,0:T(8,128)} fusion(f32[4,32,64,128]{3,2,1,0:T(8,128)S(1)} %multiply_add_fusion.1, f32[4,32,64,128]{3,2,1,0:T(8,128)S(1)} %copy-done, f32[6,34,1,128]{3,2,1,0:T(1,128)S(1)} %copy.31, f32[6,1,64,128]{3,2,1,0:T(8,128)S(1)} %collective-permute-done.14, f32[1,32,64,128]{3,2,1,0:T(8,128)S(1)} %collective-permute-done.12, ...), kind=kLoop, calls=%fused_computation.46 | loop fusion | flops 37748736 | bytes 23670784 | tf_op jit(solution)/shard_map/add | solution.py:42
  (41 shorter events, 11.0 us)
Async XLA Ops:
  0.0 6.7 %copy-start.4 = (f32[4,32,64,128]{3,2,1,0:T(8,128)S(1)}, f32[4,32,64,128]{3,2,1,0:T(8,128)}, u32[]{:S(2)}) copy-start(f32[4,32,64,128]{3,2,1,0:T(8,128)} %param.4) | copy-start | bytes 12582916
  1.8 4.8 %collective-permute-start.1 = (f32[1,32,64,128]{3,2,1,0:T(8,128)S(1)}, f32[1,32,64,128]{3,2,1,0:T(8,128)S(1)}, u32[]{:S(2)}, u32[]{:S(2)}) collective-permute-start(f32[1,32,64,128]{3,2,1,0:T(8,128)S(1)} %get-tuple-element.22), channel_id=1, source_target_pairs={{0,16},{1,17},{2,18},{3,19},{4,20},{5,21},{6,22},{7,23},{8,24},{9,... | collective-permute-start | bytes 3145736 | tf_op jit(solution)/shard_map/ppermute | solution.py:16
  4.4 4.6 %collective-permute-start = (f32[1,32,64,128]{3,2,1,0:T(8,128)S(1)}, f32[1,32,64,128]{3,2,1,0:T(8,128)S(1)}, u32[]{:S(2)}, u32[]{:S(2)}) collective-permute-start(f32[1,32,64,128]{3,2,1,0:T(8,128)S(1)} %get-tuple-element.21), channel_id=1, source_target_pairs={{16,0},{17,1},{18,2},{19,3},{20,4},{21,5},{22,6},{23,7},{24,8},{25... | collective-permute-start | bytes 3145736 | tf_op jit(solution)/shard_map/ppermute | solution.py:17
  9.1 21.4 %copy-start.3 = (f32[6,32,64,128]{3,2,1,0:T(8,128)}, f32[6,32,64,128]{3,2,1,0:T(8,128)S(1)}, u32[]{:S(2)}) copy-start(f32[6,32,64,128]{3,2,1,0:T(8,128)S(1)} %constant_dynamic-update-slice_fusion) | copy-start | bytes 18874372
  9.1 8.8 %collective-permute-start.3 = (f32[6,1,64,128]{3,2,1,0:T(8,128)S(1)}, f32[6,1,64,128]{3,2,1,0:T(8,128)S(1)}, u32[]{:S(2)}, u32[]{:S(2)}) collective-permute-start(f32[6,1,64,128]{3,2,1,0:T(8,128)S(1)} %get-tuple-element.15), channel_id=1, source_target_pairs={{0,4},{4,8},{8,12},{1,5},{5,9},{9,13},{2,6},{6,10},{10,14},{3,7},{... | collective-permute-start | bytes 589832 | tf_op jit(solution)/shard_map/ppermute | solution.py:16
  13.4 8.6 %collective-permute-start.2 = (f32[6,1,64,128]{3,2,1,0:T(8,128)S(1)}, f32[6,1,64,128]{3,2,1,0:T(8,128)S(1)}, u32[]{:S(2)}, u32[]{:S(2)}) collective-permute-start(f32[6,1,64,128]{3,2,1,0:T(8,128)S(1)} %get-tuple-element.16), channel_id=1, source_target_pairs={{4,0},{8,4},{12,8},{5,1},{9,5},{13,9},{6,2},{10,6},{14,10},{7,3},{... | collective-permute-start | bytes 589832 | tf_op jit(solution)/shard_map/ppermute | solution.py:17
  22.2 6.8 %collective-permute-start.4 = (f32[6,34,1,128]{3,1,2,0:T(8,128)S(1)}, f32[6,34,1,128]{3,1,2,0:T(8,128)S(1)}, u32[]{:S(2)}, u32[]{:S(2)}) collective-permute-start(f32[6,34,1,128]{3,1,2,0:T(8,128)S(1)} %copy.22), channel_id=1, source_target_pairs={{2,0},{3,1},{6,4},{7,5},{10,8},{11,9},{14,12},{15,13},{18,16},{19,... | collective-permute-start | bytes 313352 | tf_op jit(solution)/shard_map/ppermute | solution.py:17
  23.5 7.0 %collective-permute-start.5 = (f32[6,34,1,128]{3,1,2,0:T(8,128)S(1)}, f32[6,34,1,128]{3,1,2,0:T(8,128)S(1)}, u32[]{:S(2)}, u32[]{:S(2)}) collective-permute-start(f32[6,34,1,128]{3,1,2,0:T(8,128)S(1)} %copy.24), channel_id=1, source_target_pairs={{0,2},{1,3},{4,6},{5,7},{8,10},{9,11},{12,14},{13,15},{16,18},{17,... | collective-permute-start | bytes 313352 | tf_op jit(solution)/shard_map/ppermute | solution.py:16
  47.9 3.6 %collective-permute-start.7 = (f32[1,32,64,128]{3,2,1,0:T(8,128)S(1)}, f32[1,32,64,128]{3,2,1,0:T(8,128)S(1)}, u32[]{:S(2)}, u32[]{:S(2)}) collective-permute-start(f32[1,32,64,128]{3,2,1,0:T(8,128)S(1)} %get-tuple-element.19), channel_id=1, source_target_pairs={{0,16},{1,17},{2,18},{3,19},{4,20},{5,21},{6,22},{7,23},{8,24},{9,... | collective-permute-start | bytes 3145736 | tf_op jit(solution)/shard_map/ppermute | solution.py:16
  49.3 4.6 %collective-permute-start.6 = (f32[1,32,64,128]{3,2,1,0:T(8,128)S(1)}, f32[1,32,64,128]{3,2,1,0:T(8,128)S(1)}, u32[]{:S(2)}, u32[]{:S(2)}) collective-permute-start(f32[1,32,64,128]{3,2,1,0:T(8,128)S(1)} %get-tuple-element.20), channel_id=1, source_target_pairs={{16,0},{17,1},{18,2},{19,3},{20,4},{21,5},{22,6},{23,7},{24,8},{25... | collective-permute-start | bytes 3145736 | tf_op jit(solution)/shard_map/ppermute | solution.py:17
  53.8 21.1 %copy-start.1 = (f32[4,32,64,128]{3,2,1,0:T(8,128)S(1)}, f32[4,32,64,128]{3,2,1,0:T(8,128)}, u32[]{:S(2)}) copy-start(f32[4,32,64,128]{3,2,1,0:T(8,128)} %param.6) | copy-start | bytes 12582916
  53.8 21.1 %copy-start.2 = (f32[4,32,64,128]{3,2,1,0:T(8,128)S(1)}, f32[4,32,64,128]{3,2,1,0:T(8,128)}, u32[]{:S(2)}) copy-start(f32[4,32,64,128]{3,2,1,0:T(8,128)} %param.5) | copy-start | bytes 12582916
  53.9 21.1 %copy-start = (f32[4,32,64,128]{3,2,1,0:T(8,128)S(1)}, f32[4,32,64,128]{3,2,1,0:T(8,128)}, u32[]{:S(2)}) copy-start(f32[4,32,64,128]{3,2,1,0:T(8,128)} %param.7) | copy-start | bytes 12582916
  53.9 8.3 %collective-permute-start.9 = (f32[6,1,64,128]{3,2,1,0:T(8,128)S(1)}, f32[6,1,64,128]{3,2,1,0:T(8,128)S(1)}, u32[]{:S(2)}, u32[]{:S(2)}) collective-permute-start(f32[6,1,64,128]{3,2,1,0:T(8,128)S(1)} %get-tuple-element.13), channel_id=1, source_target_pairs={{0,4},{4,8},{8,12},{1,5},{5,9},{9,13},{2,6},{6,10},{10,14},{3,7},{... | collective-permute-start | bytes 589832 | tf_op jit(solution)/shard_map/ppermute | solution.py:16
  57.8 8.6 %collective-permute-start.8 = (f32[6,1,64,128]{3,2,1,0:T(8,128)S(1)}, f32[6,1,64,128]{3,2,1,0:T(8,128)S(1)}, u32[]{:S(2)}, u32[]{:S(2)}) collective-permute-start(f32[6,1,64,128]{3,2,1,0:T(8,128)S(1)} %get-tuple-element.14), channel_id=1, source_target_pairs={{4,0},{8,4},{12,8},{5,1},{9,5},{13,9},{6,2},{10,6},{14,10},{7,3},{... | collective-permute-start | bytes 589832 | tf_op jit(solution)/shard_map/ppermute | solution.py:17
  66.5 6.8 %collective-permute-start.10 = (f32[6,34,1,128]{3,1,2,0:T(8,128)S(1)}, f32[6,34,1,128]{3,1,2,0:T(8,128)S(1)}, u32[]{:S(2)}, u32[]{:S(2)}) collective-permute-start(f32[6,34,1,128]{3,1,2,0:T(8,128)S(1)} %copy.26), channel_id=1, source_target_pairs={{2,0},{3,1},{6,4},{7,5},{10,8},{11,9},{14,12},{15,13},{18,16},{19,... | collective-permute-start | bytes 313352 | tf_op jit(solution)/shard_map/ppermute | solution.py:17
  67.8 7.0 %collective-permute-start.11 = (f32[6,34,1,128]{3,1,2,0:T(8,128)S(1)}, f32[6,34,1,128]{3,1,2,0:T(8,128)S(1)}, u32[]{:S(2)}, u32[]{:S(2)}) collective-permute-start(f32[6,34,1,128]{3,1,2,0:T(8,128)S(1)} %copy.28), channel_id=1, source_target_pairs={{0,2},{1,3},{4,6},{5,7},{8,10},{9,11},{12,14},{13,15},{16,18},{17,... | collective-permute-start | bytes 313352 | tf_op jit(solution)/shard_map/ppermute | solution.py:16
  83.1 3.6 %collective-permute-start.13 = (f32[1,32,64,128]{3,2,1,0:T(8,128)S(1)}, f32[1,32,64,128]{3,2,1,0:T(8,128)S(1)}, u32[]{:S(2)}, u32[]{:S(2)}) collective-permute-start(f32[1,32,64,128]{3,2,1,0:T(8,128)S(1)} %get-tuple-element.17), channel_id=1, source_target_pairs={{0,16},{1,17},{2,18},{3,19},{4,20},{5,21},{6,22},{7,23},{8,24},{9,... | collective-permute-start | bytes 3145736 | tf_op jit(solution)/shard_map/ppermute | solution.py:16
  84.5 4.6 %collective-permute-start.12 = (f32[1,32,64,128]{3,2,1,0:T(8,128)S(1)}, f32[1,32,64,128]{3,2,1,0:T(8,128)S(1)}, u32[]{:S(2)}, u32[]{:S(2)}) collective-permute-start(f32[1,32,64,128]{3,2,1,0:T(8,128)S(1)} %get-tuple-element.18), channel_id=1, source_target_pairs={{16,0},{17,1},{18,2},{19,3},{20,4},{21,5},{22,6},{23,7},{24,8},{25... | collective-permute-start | bytes 3145736 | tf_op jit(solution)/shard_map/ppermute | solution.py:17
  89.1 7.9 %collective-permute-start.15 = (f32[6,1,64,128]{3,2,1,0:T(8,128)S(1)}, f32[6,1,64,128]{3,2,1,0:T(8,128)S(1)}, u32[]{:S(2)}, u32[]{:S(2)}) collective-permute-start(f32[6,1,64,128]{3,2,1,0:T(8,128)S(1)} %get-tuple-element.11), channel_id=1, source_target_pairs={{0,4},{4,8},{8,12},{1,5},{5,9},{9,13},{2,6},{6,10},{10,14},{3,7},{... | collective-permute-start | bytes 589832 | tf_op jit(solution)/shard_map/ppermute | solution.py:16
  92.6 8.6 %collective-permute-start.14 = (f32[6,1,64,128]{3,2,1,0:T(8,128)S(1)}, f32[6,1,64,128]{3,2,1,0:T(8,128)S(1)}, u32[]{:S(2)}, u32[]{:S(2)}) collective-permute-start(f32[6,1,64,128]{3,2,1,0:T(8,128)S(1)} %get-tuple-element.12), channel_id=1, source_target_pairs={{4,0},{8,4},{12,8},{5,1},{9,5},{13,9},{6,2},{10,6},{14,10},{7,3},{... | collective-permute-start | bytes 589832 | tf_op jit(solution)/shard_map/ppermute | solution.py:17
  101.3 6.8 %collective-permute-start.16 = (f32[6,34,1,128]{3,1,2,0:T(8,128)S(1)}, f32[6,34,1,128]{3,1,2,0:T(8,128)S(1)}, u32[]{:S(2)}, u32[]{:S(2)}) collective-permute-start(f32[6,34,1,128]{3,1,2,0:T(8,128)S(1)} %copy.30), channel_id=1, source_target_pairs={{2,0},{3,1},{6,4},{7,5},{10,8},{11,9},{14,12},{15,13},{18,16},{19,... | collective-permute-start | bytes 313352 | tf_op jit(solution)/shard_map/ppermute | solution.py:17
  102.6 7.0 %collective-permute-start.17 = (f32[6,34,1,128]{3,1,2,0:T(8,128)S(1)}, f32[6,34,1,128]{3,1,2,0:T(8,128)S(1)}, u32[]{:S(2)}, u32[]{:S(2)}) collective-permute-start(f32[6,34,1,128]{3,1,2,0:T(8,128)S(1)} %copy.32), channel_id=1, source_target_pairs={{0,2},{1,3},{4,6},{5,7},{8,10},{9,11},{12,14},{13,15},{16,18},{17,... | collective-permute-start | bytes 313352 | tf_op jit(solution)/shard_map/ppermute | solution.py:16
where the time goes:
time: 119 us; the launch traced here: 118 us
  starting transfers between devices  42.3 us (36%)
  waiting for transfers between devices  37.1 us (31%)
  other arithmetic  33.8 us (28%)
  local copies, waits for them, and re-layouts  4.86 us (4%)
    add x3, other arithmetic, advance(): middle - flow_j * slopes[0] - flow_i * slopes[1] - flow_k * slopes[2]  33.3 us
    ppermute x9, starting transfers between devices, padded_2(): before = lax.ppermute(last, axis, up)  30.6 us
    ppermute x9, waiting for transfers between devices, padded_2(): after = lax.ppermute(initial, axis, down)  21.4 us
    ppermute x9, waiting for transfers between devices, padded_2(): before = lax.ppermute(last, axis, up)  15.7 us
    ppermute x9, starting transfers between devices, padded_2(): after = lax.ppermute(initial, axis, down)  11.6 us
  transfers between devices with their start and end apart: 18, of which 18 were waited for; matrix products, arithmetic and copies ran while one was open for 1% of the time, Pallas kernels for 0%

commit v1 on v0

v1 whole, which is shorter than its diff:
```python
import functools

import jax
import jax.numpy as jnp
from jax import lax
from jax.experimental import pallas as pl
from jax.experimental.pallas import tpu as pltpu
from jax.sharding import PartitionSpec as P

STEPS = 3
AXES = ("south", "east", "down")
RATE = 0.05


def exchange(axis, faces):
    count = lax.axis_size(axis)
    if len(faces) == 1:
        return [lax.ppermute(faces[0], axis, [(0, 1), (1, 0)])]
    up = [(i, i + 1) for i in range(count - 1)]
    first, last = faces
    return [lax.ppermute(last, axis, up), lax.ppermute(first, axis, [(j, i) for i, j in up])]


def main_kernel(d_ref, fj_ref, fi_ref, fk_ref, o_ref):
    nj, ni, nk, _ = d_ref.shape
    row = lax.broadcasted_iota(jnp.int32, d_ref.shape[2:], 0)

    for j in range(nj):

        @pl.loop(0, ni)
        def _(i, j=j):
            m = d_ref[j, i]
            below = jnp.maximum(i - 1, 0)
            above = jnp.minimum(i + 1, ni - 1)
            lo = jnp.where(i > 0, RATE, 0.0)
            hi = jnp.where(i < ni - 1, RATE, 0.0)
            lo1 = jnp.where(i > 0, 1.0, 0.0)
            hi1 = jnp.where(i < ni - 1, 1.0, 0.0)
            im = d_ref[j, below] * lo1
            ip = d_ref[j, above] * hi1
            km = jnp.where(row == 0, 0.0, pltpu.roll(m, 1, 0))
            kp = jnp.where(row == nk - 1, 0.0, pltpu.roll(m, nk - 1, 0))
            total = im + ip + (km + kp)
            out = m - fi_ref[j, i] * (ip - im) - fk_ref[j, i] * (kp - km)
            fj = fj_ref[j, i]
            if j > 0 and j < nj - 1:
                jm, jp = d_ref[j - 1, i], d_ref[j + 1, i]
                total = total + (jm + jp)
                out = out - fj * (jp - jm)
            elif j > 0:
                jm = d_ref[j - 1, i]
                total = total + jm
                out = out + fj * jm
            elif nj > 1:
                jp = d_ref[j + 1, i]
                total = total + jp
                out = out - fj * jp
            o_ref[j, i] = out + RATE * (total - 6.0 * m)


def patch_kernel(counts, emit, *refs):
    d_ref, fj_ref, fi_ref, fk_ref = refs[:4]
    at = 4
    halos = []
    for count in counts:
        size = 1 if count == 2 else 2 if count > 2 else 0
        halos.append(refs[at : at + size])
        at += size
    o_ref = refs[at]
    faces, at = [], at + 1
    if emit:
        for halo in halos:
            faces.append(refs[at : at + len(halo)])
            at += len(halo)
    nj, ni, nk, _ = d_ref.shape

    def sides(dim, length, step=1):
        count, halo = counts[dim], halos[dim]
        face = faces[dim] if emit else (None,) * len(halo)
        if count == 2:
            upper = lax.axis_index(AXES[dim]) == 0
            return [(jnp.where(upper, length - step, 0), jnp.where(upper, -1.0, 1.0), halo[0], face[0])]
        if count > 2:
            return [(0, 1.0, halo[0], face[0]), (length - step, -1.0, halo[1], face[1])]
        return []

    tile = 8
    row = lax.broadcasted_iota(jnp.int32, (tile, d_ref.shape[3]), 0)
    for start, sign, halo, _ in sides(2, nk, tile):
        start = pl.multiple_of(start, tile) if not isinstance(start, int) else start
        own = jnp.where(sign > 0, 0, tile - 1) if not isinstance(sign, float) else (0 if sign > 0 else tile - 1)
        mask = jnp.where(row == own, 1.0, 0.0)
        for j in range(nj):

            @pl.loop(0, ni, unroll=8)
            def _(i, j=j):
                weight = (RATE + sign * fk_ref[j, i, pl.ds(start, tile)]) * mask
                o_ref[j, i, pl.ds(start, tile)] = d_ref[j, i, pl.ds(start, tile)] + weight * halo[j, pl.ds(i, 1)]

    for at_i, sign, halo, _ in sides(1, ni):
        for j in range(nj):
            o_ref[j, at_i] = o_ref[j, at_i] + (RATE + sign * fi_ref[j, at_i]) * halo[j]
    for at_j, sign, halo, face in sides(0, nj):

        @pl.loop(0, ni)
        def _(i, at_j=at_j, sign=sign, halo=halo, face=face):
            out = o_ref[at_j, i] + (RATE + sign * fj_ref[at_j, i]) * halo[i]
            o_ref[at_j, i] = out

    if emit:
        for dim, length in ((0, nj), (1, ni), (2, nk)):
            for at_d, _, _, face in sides(dim, length):
                if dim == 0:

                    @pl.loop(0, ni)
                    def _(i, at_d=at_d, face=face):
                        face[i] = o_ref[at_d, i]

                elif dim == 1:
                    for j in range(nj):
                        face[j] = o_ref[j, at_d]
                else:
                    for j in range(nj):

                        @pl.loop(0, ni, unroll=8)
                        def _(i, j=j, at_d=at_d, face=face):
                            face[j, pl.ds(i, 1)] = o_ref[j, i, pl.ds(at_d, 1)]


VM = pl.BlockSpec(memory_space=pltpu.VMEM)


def per_device(density, flow_j, flow_i, flow_k):
    counts = [lax.axis_size(axis) for axis in AXES]
    shape, dtype = density.shape, density.dtype
    cells = density.size
    face_shapes = [shape[:d] + shape[d + 1 :] for d in range(3)]
    flows = (flow_j, flow_i, flow_k)
    limit = 24 * 2**20

    def first_faces(x):
        out = []
        for dim, (axis, count) in enumerate(zip(AXES, counts)):
            n = shape[dim]
            if count == 2:
                start = jnp.where(lax.axis_index(axis) == 0, n - 1, 0)
                out.append([lax.dynamic_index_in_dim(x, start, dim, keepdims=False)])
            elif count > 2:
                out.append([lax.index_in_dim(x, at, dim, keepdims=False) for at in (0, n - 1)])
            else:
                out.append([])
        return out

    def swap_order(faces):
        halos = [None] * 3
        for dim in (1, 0, 2):
            halos[dim] = exchange(AXES[dim], faces[dim]) if faces[dim] else []
        return halos

    main = pl.pallas_call(
        main_kernel,
        out_shape=pltpu.VMEM(shape, dtype),
        in_specs=[VM] * 4,
        out_specs=VM,
        name="main",
        compiler_params=pltpu.CompilerParams(vmem_limit_bytes=limit),
        cost_estimate=pl.CostEstimate(flops=24 * cells, bytes_accessed=20 * cells, transcendentals=0),
    )

    def patch(x, halos, emit):
        flat = [h for hs in halos for h in hs]
        outs = [pltpu.VMEM(shape, dtype)]
        if emit:
            outs += [pltpu.VMEM(face_shapes[d], dtype) for d in range(3) for _ in halos[d]]
        got = pl.pallas_call(
            functools.partial(patch_kernel, counts, emit),
            out_shape=outs,
            in_specs=[VM] * (4 + len(flat)),
            out_specs=[VM] * len(outs),
            input_output_aliases={0: 0},
            name="patch",
            compiler_params=pltpu.CompilerParams(vmem_limit_bytes=limit),
            cost_estimate=pl.CostEstimate(flops=cells, bytes_accessed=cells, transcendentals=0),
        )(x, *flows, *flat)
        x, rest, faces = got[0], list(got[1:]), []
        for d in range(3):
            size = len(halos[d]) if emit else 0
            faces.append(rest[:size])
            rest = rest[size:]
        return x, faces

    faces = first_faces(density)
    for step in range(STEPS):
        halos = swap_order(faces)
        density = main(density, *flows)
        density, faces = patch(density, halos, step < STEPS - 1)
    return density


def solution(mesh):
    spec = P(("ens", "south"), "east", "down", None)
    return jax.shard_map(per_device, mesh=mesh, in_specs=(spec,) * 4, out_specs=spec, check_vma=False)
```

time: 119 us -> 53.4 us (0.45)
  waiting for transfers between devices: 37.1 us -> 2.72 us
  other arithmetic: 33.8 us -> 0 us
  starting transfers between devices: 42.3 us -> 20.3 us
  Pallas kernels: 0 us -> 14.9 us
  local copies, waits for them, and re-layouts: 4.86 us -> 14.7 us
    ppermute x18 -> x12, waiting for transfers between devices: 37.1 us -> 2.72 us  [the longest x3 2.69 us: exchange(): lax.ppermute(first, axis, [(j, i) for i, j in up])]
    add x3 -> x0, other arithmetic: 33.3 us -> none  [advance(): middle - flow_j * slopes[0] - flow_i * slopes[1] - flow_k * slopes[2]]
    ppermute x18 -> x12, starting transfers between devices: 42.3 us -> 20.3 us  [the longest x3 12.1 us: exchange(): lax.ppermute(last, axis, up)]
    pallas_call x0 -> x6, Pallas kernels: none -> 14.9 us  [the longest x3 12 us: per_device(): density = main(density, *flows)]
    unnamed x12 -> x15, local copies, waits for them, and re-layouts: 0.67 us -> 11.4 us
    squeeze x0 -> x2, local copies, waits for them, and re-layouts: none -> 2.28 us  [the longest x1 1.29 us: first_faces(): out.append([lax.dynamic_index_in_dim(x, start, dim, keepdims=False)])]
    slice x10 -> x0, local copies, waits for them, and re-layouts: 2.19 us -> none  [the longest x4 1.86 us: padded_2(): initial = lax.slice_in_dim(x, 0, width, axis=dim)]
    ppermute x6 -> x0, local copies, waits for them, and re-layouts: 1.93 us -> none  [the longest x3 0.97 us: padded_2(): before = lax.ppermute(last, axis, up)]
  transfers between devices with their start and end apart: 18 -> 12, of which waited for: 18 -> 2; matrix products, arithmetic and copies ran while one was open for 1% -> 4% of each run, Pallas kernels for 0% -> 23%
where the time goes in v1:
time: 53.4 us; the launch traced here: 52.9 us
  starting transfers between devices  20.3 us (38%)
  Pallas kernels  14.9 us (28%)
  local copies, waits for them, and re-layouts  14.7 us (28%)
  waiting for transfers between devices  2.72 us (5%)
    ppermute x3, starting transfers between devices, exchange(): lax.ppermute(last, axis, up)  12.1 us
    pallas_call x3, Pallas kernels, per_device(): density = main(density, *flows)  12 us
    unnamed x15, local copies, waits for them, and re-layouts  11.4 us
    ppermute x6, starting transfers between devices, exchange(): return [lax.ppermute(faces[0], axis, [(0, 1), (1, 0)])]  4.37 us
    ppermute x3, starting transfers between devices, exchange(): lax.ppermute(first, axis, [(j, i) for i, j in up])  3.88 us
    pallas_call x3, Pallas kernels, patch(): pl.pallas_call(functools.partial(patch_kernel, counts, emit), out_shape=o...  2.96 us
    ppermute x3, waiting for transfers between devices, exchange(): lax.ppermute(first, axis, [(j, i) for i, j in up])  2.69 us
    squeeze x1, local copies, waits for them, and re-layouts, first_faces(): out.append([lax.dynamic_index_in_dim(x, start, dim, keepdims=False)])  1.29 us
  transfers between devices with their start and end apart: 12, of which 2 were waited for; matrix products, arithmetic and copies ran while one was open for 4% of the time, Pallas kernels for 23%

profile of v1, /device:TPU:0, one launch (start us, length us, event | category | flops | bytes accessed | tf_op | source)
XLA Modules:
  0.0 52.9 jit_solution(17108279617469874951)
XLA Ops:
  0.0 1.3 %dynamic-slice_bitcast_fusion = f32[32,64,128]{2,1,0:T(8,128)S(1)} fusion(f32[4,32,64,128]{3,2,1,0:T(8,128)} %d_ref.1, s32[]{:T(128)S(6)} %select_n.11), kind=kLoop, calls=%fused_computation | loop fusion | bytes 2097156 | tf_op jit(solution)/shard_map/jit(dynamic_index_in_dim)/squeeze | solution.py:147
  1.3 0.6 %collective-permute-start = (f32[32,64,128]{2,1,0:T(8,128)S(1)}, f32[32,64,128]{2,1,0:T(8,128)S(1)}, u32[]{:S(2)}, u32[]{:S(2)}) collective-permute-start(f32[32,64,128]{2,1,0:T(8,128)S(1)} %dynamic-slice_bitcast_fusion), channel_id=1, source_target_pairs={{0,16},{16,0},{1,17},{17,1},{2,18},{18,2},{3,19},{19,3},{4,20},{20... | collective-permute-start | bytes 3145736 | tf_op jit(solution)/shard_map/ppermute | solution.py:18
  1.9 1.0 %slice_bitcast_fusion = (f32[4,64,128]{2,1,0:T(8,128)S(1)}, f32[4,64,128]{2,1,0:T(8,128)S(1)}) fusion(f32[4,32,64,128]{3,2,1,0:T(8,128)} %d_ref.1), kind=kLoop, calls=%fused_computation.1 | loop fusion | bytes 524288 | tf_op jit(solution)/shard_map/squeeze | solution.py:149
  2.8 1.3 %collective-permute-start.2 = (f32[4,64,128]{2,1,0:T(8,128)S(1)}, f32[4,64,128]{2,1,0:T(8,128)S(1)}, u32[]{:S(2)}, u32[]{:S(2)}) collective-permute-start(f32[4,64,128]{2,1,0:T(8,128)S(1)} %get-tuple-element.25), channel_id=1, source_target_pairs={{4,0},{8,4},{12,8},{5,1},{9,5},{13,9},{6,2},{10,6},{14,10},{7,3},{... | collective-permute-start | bytes 393224 | tf_op jit(solution)/shard_map/ppermute | solution.py:21
  4.1 5.1 %collective-permute-start.1 = (f32[4,64,128]{2,1,0:T(8,128)S(1)}, f32[4,64,128]{2,1,0:T(8,128)S(1)}, u32[]{:S(2)}, u32[]{:S(2)}) collective-permute-start(f32[4,64,128]{2,1,0:T(8,128)S(1)} %get-tuple-element.26), channel_id=1, source_target_pairs={{0,4},{4,8},{8,12},{1,5},{5,9},{9,13},{2,6},{6,10},{10,14},{3,7},{... | collective-permute-start | bytes 393224 | tf_op jit(solution)/shard_map/ppermute | solution.py:21
  9.3 1.1 %constant_dynamic-slice_fusion = f32[4,32,1,128]{3,2,1,0:T(1,128)S(1)} fusion(f32[4,32,64,128]{3,2,1,0:T(8,128)} %d_ref.1, s32[]{:T(128)S(6)} %select_n.12), kind=kLoop, calls=%fused_computation.3 | loop fusion | bytes 131076 | tf_op jit(solution)/shard_map/jit(dynamic_index_in_dim)/dynamic_slice | solution.py:147
  10.4 2.0 %collective-permute-start.3 = (f32[4,32,128]{2,1,0:T(8,128)S(1)}, f32[4,32,128]{2,1,0:T(8,128)S(1)}, u32[]{:S(2)}, u32[]{:S(2)}) collective-permute-start(f32[4,32,128]{2,1,0:T(8,128)S(1)} %bitcast.11), channel_id=1, source_target_pairs={{0,2},{2,0},{1,3},{3,1},{4,6},{6,4},{5,7},{7,5},{8,10},{10,8},{9,1... | collective-permute-start | bytes 196616 | tf_op jit(solution)/shard_map/ppermute | solution.py:18
  12.4 2.2 %copy-done = f32[4,32,64,128]{3,2,1,0:T(8,128)S(1)} copy-done((f32[4,32,64,128]{3,2,1,0:T(8,128)S(1)}, f32[4,32,64,128]{3,2,1,0:T(8,128)}, u32[]{:S(2)}) %copy-start) | copy-done | bytes 4194328
  14.6 2.2 %copy-done.2 = f32[4,32,64,128]{3,2,1,0:T(8,128)S(1)} copy-done((f32[4,32,64,128]{3,2,1,0:T(8,128)S(1)}, f32[4,32,64,128]{3,2,1,0:T(8,128)}, u32[]{:S(2)}) %copy-start.2) | copy-done | bytes 4194328
  16.8 2.2 %copy-done.4 = f32[4,32,64,128]{3,2,1,0:T(8,128)S(1)} copy-done((f32[4,32,64,128]{3,2,1,0:T(8,128)S(1)}, f32[4,32,64,128]{3,2,1,0:T(8,128)}, u32[]{:S(2)}) %copy-start.4) | copy-done | bytes 4194328
  18.9 2.2 %copy-done.6 = f32[4,32,64,128]{3,2,1,0:T(8,128)S(1)} copy-done((f32[4,32,64,128]{3,2,1,0:T(8,128)S(1)}, f32[4,32,64,128]{3,2,1,0:T(8,128)}, u32[]{:S(2)}) %copy-start.6) | copy-done | bytes 4194328
  21.1 4.0 %main.3.refs_0_ = f32[4,32,64,128]{3,2,1,0:T(8,128)S(1)} custom-call(f32[4,32,64,128]{3,2,1,0:T(8,128)S(1)} %copy-done.6, f32[4,32,64,128]{3,2,1,0:T(8,128)S(1)} %copy-done, f32[4,32,64,128]{3,2,1,0:T(8,128)S(1)} %copy-done.2, f32[4,32,64,128]{3,2,1,0:T(8,128)S(1)} %copy-done.4), custom_call_target="tpu_custom_call" | custom-call | flops 25165824 | bytes 20971520 | tf_op jit(solution)/shard_map/main/pallas_call | solution.py:195
  25.1 0.0 collective-permute-done.3.refs_7_
  25.1 0.0 collective-permute-done.2.refs_6_
  25.2 0.0 collective-permute-done.refs_4_
  25.2 0.6 %copy-done.5 = f32[4,32,64,128]{3,2,1,0:T(8,128)S(1)} copy-done((f32[4,32,64,128]{3,2,1,0:T(8,128)S(1)}, f32[4,32,64,128]{3,2,1,0:T(8,128)}, u32[]{:S(2)}) %copy-start.5) | copy-done | bytes 4194328
  25.8 1.1 %patch.3 = (f32[4,32,64,128]{3,2,1,0:T(8,128)S(1)}, f32[32,64,128]{2,1,0:T(8,128)S(1)}, f32[4,64,128]{2,1,0:T(8,128)S(1)}, f32[4,64,128]{2,1,0:T(8,128)S(1)}, f32[4,32,128]{2,1,0:T(8,128)S(1)}) custom-call(f32[4,32,64,128]{3,2,1,0:T(8,128)S(1)} %main.3.refs_0_, f32[4,32,64,128]{3,2,1,0:T(8,128)S(1)} %copy-done.1, ...), custom_call_target="tpu_custom_call", output_to_operand_aliasing={{0}: (0, {})} | custom-call | flops 1048576 | bytes 1048576 | tf_op jit(solution)/shard_map/patch/pallas_call | solution.py:175
  26.9 0.1 collective-permute-start.4
  27.0 3.5 %collective-permute-start.5 = (f32[4,64,128]{2,1,0:T(8,128)S(1)}, f32[4,64,128]{2,1,0:T(8,128)S(1)}, u32[]{:S(2)}, u32[]{:S(2)}) collective-permute-start(f32[4,64,128]{2,1,0:T(8,128)S(1)} %get-tuple-element.17), channel_id=1, source_target_pairs={{0,4},{4,8},{8,12},{1,5},{5,9},{9,13},{2,6},{6,10},{10,14},{3,7},{... | collective-permute-start | bytes 393224 | tf_op jit(solution)/shard_map/ppermute | solution.py:21
  30.5 1.3 %collective-permute-start.6 = (f32[4,64,128]{2,1,0:T(8,128)S(1)}, f32[4,64,128]{2,1,0:T(8,128)S(1)}, u32[]{:S(2)}, u32[]{:S(2)}) collective-permute-start(f32[4,64,128]{2,1,0:T(8,128)S(1)} %get-tuple-element.18), channel_id=1, source_target_pairs={{4,0},{8,4},{12,8},{5,1},{9,5},{13,9},{6,2},{10,6},{14,10},{7,3},{... | collective-permute-start | bytes 393224 | tf_op jit(solution)/shard_map/ppermute | solution.py:21
  31.8 0.6 %collective-permute-start.7 = (f32[4,32,128]{2,1,0:T(8,128)S(1)}, f32[4,32,128]{2,1,0:T(8,128)S(1)}, u32[]{:S(2)}, u32[]{:S(2)}) collective-permute-start(f32[4,32,128]{2,1,0:T(8,128)S(1)} %get-tuple-element.19), channel_id=1, source_target_pairs={{0,2},{2,0},{1,3},{3,1},{4,6},{6,4},{5,7},{7,5},{8,10},{10,8},{9,1... | collective-permute-start | bytes 196616 | tf_op jit(solution)/shard_map/ppermute | solution.py:18
  32.4 4.0 %main.4.refs_0_ = f32[4,32,64,128]{3,2,1,0:T(8,128)S(1)} custom-call(f32[4,32,64,128]{3,2,1,0:T(8,128)S(1)} %get-tuple-element.15.d_ref, f32[4,32,64,128]{3,2,1,0:T(8,128)S(1)} %copy-done.1, f32[4,32,64,128]{3,2,1,0:T(8,128)S(1)} %copy-done.3, f32[4,32,64,128]{3,2,1,0:T(8,128)S(1)} %copy-done.5), custom_call_target="tpu_custom_call" | custom-call | flops 25165824 | bytes 20971520 | tf_op jit(solution)/shard_map/main/pallas_call | solution.py:195
  36.4 1.6 %collective-permute-done.6.refs_6_ = f32[4,64,128]{2,1,0:T(8,128)S(1)} collective-permute-done((f32[4,64,128]{2,1,0:T(8,128)S(1)}, f32[4,64,128]{2,1,0:T(8,128)S(1)}, u32[]{:S(2)}, u32[]{:S(2)}) %collective-permute-start.6) | collective-permute-done | bytes 131104 | tf_op jit(solution)/shard_map/ppermute | solution.py:21
  38.0 1.1 %patch.4 = (f32[4,32,64,128]{3,2,1,0:T(8,128)S(1)}, f32[32,64,128]{2,1,0:T(8,128)S(1)}, f32[4,64,128]{2,1,0:T(8,128)S(1)}, f32[4,64,128]{2,1,0:T(8,128)S(1)}, f32[4,32,128]{2,1,0:T(8,128)S(1)}) custom-call(f32[4,32,64,128]{3,2,1,0:T(8,128)S(1)} %main.4.refs_0_, f32[4,32,64,128]{3,2,1,0:T(8,128)S(1)} %copy-done.1, ...), custom_call_target="tpu_custom_call", output_to_operand_aliasing={{0}: (0, {})} | custom-call | flops 1048576 | bytes 1048576 | tf_op jit(solution)/shard_map/patch/pallas_call | solution.py:175
  39.1 0.1 collective-permute-start.8
  39.2 3.5 %collective-permute-start.9 = (f32[4,64,128]{2,1,0:T(8,128)S(1)}, f32[4,64,128]{2,1,0:T(8,128)S(1)}, u32[]{:S(2)}, u32[]{:S(2)}) collective-permute-start(f32[4,64,128]{2,1,0:T(8,128)S(1)} %get-tuple-element.22), channel_id=1, source_target_pairs={{0,4},{4,8},{8,12},{1,5},{5,9},{9,13},{2,6},{6,10},{10,14},{3,7},{... | collective-permute-start | bytes 393224 | tf_op jit(solution)/shard_map/ppermute | solution.py:21
  42.7 1.3 %collective-permute-start.10 = (f32[4,64,128]{2,1,0:T(8,128)S(1)}, f32[4,64,128]{2,1,0:T(8,128)S(1)}, u32[]{:S(2)}, u32[]{:S(2)}) collective-permute-start(f32[4,64,128]{2,1,0:T(8,128)S(1)} %get-tuple-element.23), channel_id=1, source_target_pairs={{4,0},{8,4},{12,8},{5,1},{9,5},{13,9},{6,2},{10,6},{14,10},{7,3},{... | collective-permute-start | bytes 393224 | tf_op jit(solution)/shard_map/ppermute | solution.py:21
  44.0 1.1 %collective-permute-start.11 = (f32[4,32,128]{2,1,0:T(8,128)S(1)}, f32[4,32,128]{2,1,0:T(8,128)S(1)}, u32[]{:S(2)}, u32[]{:S(2)}) collective-permute-start(f32[4,32,128]{2,1,0:T(8,128)S(1)} %get-tuple-element.24), channel_id=1, source_target_pairs={{0,2},{2,0},{1,3},{3,1},{4,6},{6,4},{5,7},{7,5},{8,10},{10,8},{9,1... | collective-permute-start | bytes 196616 | tf_op jit(solution)/shard_map/ppermute | solution.py:18
  45.0 4.0 %main.5.refs_0_ = f32[4,32,64,128]{3,2,1,0:T(8,128)S(1)} custom-call(f32[4,32,64,128]{3,2,1,0:T(8,128)S(1)} %get-tuple-element.20.d_ref, f32[4,32,64,128]{3,2,1,0:T(8,128)S(1)} %copy-done.1, f32[4,32,64,128]{3,2,1,0:T(8,128)S(1)} %copy-done.3, f32[4,32,64,128]{3,2,1,0:T(8,128)S(1)} %copy-done.5), custom_call_target="tpu_custom_call" | custom-call | flops 25165824 | bytes 20971520 | tf_op jit(solution)/shard_map/main/pallas_call | solution.py:195
  49.0 1.1 %collective-permute-done.10.refs_6_ = f32[4,64,128]{2,1,0:T(8,128)S(1)} collective-permute-done((f32[4,64,128]{2,1,0:T(8,128)S(1)}, f32[4,64,128]{2,1,0:T(8,128)S(1)}, u32[]{:S(2)}, u32[]{:S(2)}) %collective-permute-start.10) | collective-permute-done | bytes 131104 | tf_op jit(solution)/shard_map/ppermute | solution.py:21
  50.2 0.8 %patch.5 = f32[4,32,64,128]{3,2,1,0:T(8,128)S(1)} custom-call(f32[4,32,64,128]{3,2,1,0:T(8,128)S(1)} %main.5.refs_0_, f32[4,32,64,128]{3,2,1,0:T(8,128)S(1)} %copy-done.1, f32[4,32,64,128]{3,2,1,0:T(8,128)S(1)} %copy-done.3, f32[4,32,64,128]{3,2,1,0:T(8,128)S(1)} %copy-done.5, ...), custom_call_target="tpu_custom_call", output_to_operand_aliasing={{}: (0, {})} | custom-call | flops 1048576 | bytes 1048576 | tf_op jit(solution)/shard_map/patch/pallas_call | solution.py:175
  50.9 2.0 %copy.15 = f32[4,32,64,128]{3,2,1,0:T(8,128)} copy(f32[4,32,64,128]{3,2,1,0:T(8,128)S(1)} %patch.5) | data formatting | bytes 8388608
  (16 shorter events, 0.0 us)
Async XLA Ops:
  1.3 23.9 %collective-permute-start = (f32[32,64,128]{2,1,0:T(8,128)S(1)}, f32[32,64,128]{2,1,0:T(8,128)S(1)}, u32[]{:S(2)}, u32[]{:S(2)}) collective-permute-start(f32[32,64,128]{2,1,0:T(8,128)S(1)} %dynamic-slice_bitcast_fusion), channel_id=1, source_target_pairs={{0,16},{16,0},{1,17},{17,1},{2,18},{18,2},{3,19},{19,3},{4,20},{20... | collective-permute-start | bytes 3145736 | tf_op jit(solution)/shard_map/ppermute | solution.py:18
  2.8 22.3 %collective-permute-start.2 = (f32[4,64,128]{2,1,0:T(8,128)S(1)}, f32[4,64,128]{2,1,0:T(8,128)S(1)}, u32[]{:S(2)}, u32[]{:S(2)}) collective-permute-start(f32[4,64,128]{2,1,0:T(8,128)S(1)} %get-tuple-element.25), channel_id=1, source_target_pairs={{4,0},{8,4},{12,8},{5,1},{9,5},{13,9},{6,2},{10,6},{14,10},{7,3},{... | collective-permute-start | bytes 393224 | tf_op jit(solution)/shard_map/ppermute | solution.py:21
  4.1 21.0 %collective-permute-start.1 = (f32[4,64,128]{2,1,0:T(8,128)S(1)}, f32[4,64,128]{2,1,0:T(8,128)S(1)}, u32[]{:S(2)}, u32[]{:S(2)}) collective-permute-start(f32[4,64,128]{2,1,0:T(8,128)S(1)} %get-tuple-element.26), channel_id=1, source_target_pairs={{0,4},{4,8},{8,12},{1,5},{5,9},{9,13},{2,6},{6,10},{10,14},{3,7},{... | collective-permute-start | bytes 393224 | tf_op jit(solution)/shard_map/ppermute | solution.py:21
  10.4 14.8 %collective-permute-start.3 = (f32[4,32,128]{2,1,0:T(8,128)S(1)}, f32[4,32,128]{2,1,0:T(8,128)S(1)}, u32[]{:S(2)}, u32[]{:S(2)}) collective-permute-start(f32[4,32,128]{2,1,0:T(8,128)S(1)} %bitcast.11), channel_id=1, source_target_pairs={{0,2},{2,0},{1,3},{3,1},{4,6},{6,4},{5,7},{7,5},{8,10},{10,8},{9,1... | collective-permute-start | bytes 196616 | tf_op jit(solution)/shard_map/ppermute | solution.py:18
  12.4 2.2 %copy-start = (f32[4,32,64,128]{3,2,1,0:T(8,128)S(1)}, f32[4,32,64,128]{3,2,1,0:T(8,128)}, u32[]{:S(2)}) copy-start(f32[4,32,64,128]{3,2,1,0:T(8,128)} %refs_1_.5) | copy-start | bytes 12582916
  14.6 2.2 %copy-start.2 = (f32[4,32,64,128]{3,2,1,0:T(8,128)S(1)}, f32[4,32,64,128]{3,2,1,0:T(8,128)}, u32[]{:S(2)}) copy-start(f32[4,32,64,128]{3,2,1,0:T(8,128)} %refs_2_.5) | copy-start | bytes 12582916
  16.7 2.2 %copy-start.4 = (f32[4,32,64,128]{3,2,1,0:T(8,128)S(1)}, f32[4,32,64,128]{3,2,1,0:T(8,128)}, u32[]{:S(2)}) copy-start(f32[4,32,64,128]{3,2,1,0:T(8,128)} %refs_3_.5) | copy-start | bytes 12582916
  18.9 2.2 %copy-start.6 = (f32[4,32,64,128]{3,2,1,0:T(8,128)S(1)}, f32[4,32,64,128]{3,2,1,0:T(8,128)}, u32[]{:S(2)}) copy-start(f32[4,32,64,128]{3,2,1,0:T(8,128)} %d_ref.1) | copy-start | bytes 12582916
  21.1 4.0 %copy-start.1 = (f32[4,32,64,128]{3,2,1,0:T(8,128)S(1)}, f32[4,32,64,128]{3,2,1,0:T(8,128)}, u32[]{:S(2)}) copy-start(f32[4,32,64,128]{3,2,1,0:T(8,128)} %refs_1_.5) | copy-start | bytes 12582916
  21.1 4.1 %copy-start.3 = (f32[4,32,64,128]{3,2,1,0:T(8,128)S(1)}, f32[4,32,64,128]{3,2,1,0:T(8,128)}, u32[]{:S(2)}) copy-start(f32[4,32,64,128]{3,2,1,0:T(8,128)} %refs_2_.5) | copy-start | bytes 12582916
  21.1 4.7 %copy-start.5 = (f32[4,32,64,128]{3,2,1,0:T(8,128)S(1)}, f32[4,32,64,128]{3,2,1,0:T(8,128)}, u32[]{:S(2)}) copy-start(f32[4,32,64,128]{3,2,1,0:T(8,128)} %refs_3_.5) | copy-start | bytes 12582916
  26.9 11.1 %collective-permute-start.4 = (f32[32,64,128]{2,1,0:T(8,128)S(1)}, f32[32,64,128]{2,1,0:T(8,128)S(1)}, u32[]{:S(2)}, u32[]{:S(2)}) collective-permute-start(f32[32,64,128]{2,1,0:T(8,128)S(1)} %get-tuple-element.16), channel_id=1, source_target_pairs={{0,16},{16,0},{1,17},{17,1},{2,18},{18,2},{3,19},{19,3},{4,20},{20... | collective-permute-start | bytes 3145736 | tf_op jit(solution)/shard_map/ppermute | solution.py:18
  27.0 9.4 %collective-permute-start.5 = (f32[4,64,128]{2,1,0:T(8,128)S(1)}, f32[4,64,128]{2,1,0:T(8,128)S(1)}, u32[]{:S(2)}, u32[]{:S(2)}) collective-permute-start(f32[4,64,128]{2,1,0:T(8,128)S(1)} %get-tuple-element.17), channel_id=1, source_target_pairs={{0,4},{4,8},{8,12},{1,5},{5,9},{9,13},{2,6},{6,10},{10,14},{3,7},{... | collective-permute-start | bytes 393224 | tf_op jit(solution)/shard_map/ppermute | solution.py:21
  30.5 7.5 %collective-permute-start.6 = (f32[4,64,128]{2,1,0:T(8,128)S(1)}, f32[4,64,128]{2,1,0:T(8,128)S(1)}, u32[]{:S(2)}, u32[]{:S(2)}) collective-permute-start(f32[4,64,128]{2,1,0:T(8,128)S(1)} %get-tuple-element.18), channel_id=1, source_target_pairs={{4,0},{8,4},{12,8},{5,1},{9,5},{13,9},{6,2},{10,6},{14,10},{7,3},{... | collective-permute-start | bytes 393224 | tf_op jit(solution)/shard_map/ppermute | solution.py:21
  31.8 4.6 %collective-permute-start.7 = (f32[4,32,128]{2,1,0:T(8,128)S(1)}, f32[4,32,128]{2,1,0:T(8,128)S(1)}, u32[]{:S(2)}, u32[]{:S(2)}) collective-permute-start(f32[4,32,128]{2,1,0:T(8,128)S(1)} %get-tuple-element.19), channel_id=1, source_target_pairs={{0,2},{2,0},{1,3},{3,1},{4,6},{6,4},{5,7},{7,5},{8,10},{10,8},{9,1... | collective-permute-start | bytes 196616 | tf_op jit(solution)/shard_map/ppermute | solution.py:18
  39.1 11.1 %collective-permute-start.8 = (f32[32,64,128]{2,1,0:T(8,128)S(1)}, f32[32,64,128]{2,1,0:T(8,128)S(1)}, u32[]{:S(2)}, u32[]{:S(2)}) collective-permute-start(f32[32,64,128]{2,1,0:T(8,128)S(1)} %get-tuple-element.21), channel_id=1, source_target_pairs={{0,16},{16,0},{1,17},{17,1},{2,18},{18,2},{3,19},{19,3},{4,20},{20... | collective-permute-start | bytes 3145736 | tf_op jit(solution)/shard_map/ppermute | solution.py:18
  39.2 9.9 %collective-permute-start.9 = (f32[4,64,128]{2,1,0:T(8,128)S(1)}, f32[4,64,128]{2,1,0:T(8,128)S(1)}, u32[]{:S(2)}, u32[]{:S(2)}) collective-permute-start(f32[4,64,128]{2,1,0:T(8,128)S(1)} %get-tuple-element.22), channel_id=1, source_target_pairs={{0,4},{4,8},{8,12},{1,5},{5,9},{9,13},{2,6},{6,10},{10,14},{3,7},{... | collective-permute-start | bytes 393224 | tf_op jit(solution)/shard_map/ppermute | solution.py:21
  42.7 7.5 %collective-permute-start.10 = (f32[4,64,128]{2,1,0:T(8,128)S(1)}, f32[4,64,128]{2,1,0:T(8,128)S(1)}, u32[]{:S(2)}, u32[]{:S(2)}) collective-permute-start(f32[4,64,128]{2,1,0:T(8,128)S(1)} %get-tuple-element.23), channel_id=1, source_target_pairs={{4,0},{8,4},{12,8},{5,1},{9,5},{13,9},{6,2},{10,6},{14,10},{7,3},{... | collective-permute-start | bytes 393224 | tf_op jit(solution)/shard_map/ppermute | solution.py:21
  44.0 5.1 %collective-permute-start.11 = (f32[4,32,128]{2,1,0:T(8,128)S(1)}, f32[4,32,128]{2,1,0:T(8,128)S(1)}, u32[]{:S(2)}, u32[]{:S(2)}) collective-permute-start(f32[4,32,128]{2,1,0:T(8,128)S(1)} %get-tuple-element.24), channel_id=1, source_target_pairs={{0,2},{2,0},{1,3},{3,1},{4,6},{6,4},{5,7},{7,5},{8,10},{10,8},{9,1... | collective-permute-start | bytes 196616 | tf_op jit(solution)/shard_map/ppermute | solution.py:18

commit v2 on v0

v2 whole, which is shorter than its diff:
```python
import functools

import jax
import jax.numpy as jnp
from jax import lax
from jax.experimental import pallas as pl
from jax.experimental.pallas import tpu as pltpu
from jax.sharding import PartitionSpec as P

STEPS = 3
AXES = ("south", "east", "down")
RATE = 0.05
PIECES = 8


def rounds(count):
    return [[(i, i + 1) for i in range(begin, count - 1, 2)] for begin in range(min(2, count - 1))]


def exchange(axis, faces):
    pairs = rounds(lax.axis_size(axis))
    return [lax.ppermute(face, axis, up + [(j, i) for i, j in up]) for face, up in zip(faces, pairs)]


def sides(dim, count, length, step=1):
    out = []
    for begin in range(len(rounds(count))):
        upper = lax.axis_index(AXES[dim]) % 2 == begin
        out.append((jnp.where(upper, length - step, 0), jnp.where(upper, -1.0, 1.0)))
    return out


def copy_faces(counts, o_ref, faces, planes=None):
    nj, ni, nk, _ = o_ref.shape
    for j in range(nj) if planes is None else planes:
        for (at, _), face in zip(sides(1, counts[1], ni), faces[1]):
            face[j] = o_ref[j, at]
        for (at, _), face in zip(sides(2, counts[2], nk), faces[2]):

            @pl.loop(0, ni, unroll=8)
            def _(i, j=j, at=at, face=face):
                face[j, pl.ds(i, 1)] = o_ref[j, i, pl.ds(at, 1)]


def copy_face_j(counts, o_ref, faces):
    for (at, _), face in zip(sides(0, counts[0], o_ref.shape[0]), faces[0]):

        @pl.loop(0, o_ref.shape[1], unroll=2)
        def _(i, at=at, face=face):
            face[i] = o_ref[at, i]


def grouped(refs, counts):
    out, at = [], 0
    for count in counts:
        size = len(rounds(count))
        out.append(refs[at : at + size])
        at += size
    return out


def load_kernel(counts, x_ref, *refs):
    d_ref, sems = refs[0], refs[-1]
    faces = grouped(refs[1:-1], counts)
    copies = [pltpu.make_async_copy(x_ref.at[j], d_ref.at[j], sems.at[j]) for j in range(d_ref.shape[0])]
    for copy in copies:
        copy.start()
    for j, copy in enumerate(copies):
        copy.wait()
        copy_faces(counts, d_ref, faces, [j])
    copy_face_j(counts, d_ref, faces)


def update(d_ref, flow_refs, o_ref, i, below, above):
    fj_ref, fi_ref, fk_ref = flow_refs
    nj, _, nk, lanes = d_ref.shape
    tile = 8
    row = lax.broadcasted_iota(jnp.int32, (tile, lanes), 0)
    own = [d_ref[j, i] for j in range(nj)]

    def terms(flow, lower, upper):
        if lower is None and upper is None:
            return None
        if lower is None:
            return upper, -(flow * upper)
        if upper is None:
            return lower, flow * lower
        return lower + upper, flow * (lower - upper)

    for j in range(nj):
        m = own[j]
        km = pltpu.roll(m, 1, 0)
        kp = pltpu.roll(m, nk - 1, 0)
        km = jnp.concatenate([jnp.where(row == 0, 0.0, km[:tile]), km[tile:]], 0)
        kp = jnp.concatenate([kp[: nk - tile], jnp.where(row == tile - 1, 0.0, kp[nk - tile :])], 0)
        parts = [
            terms(fk_ref[j, i], km, kp),
            terms(fi_ref[j, i], None if below is None else d_ref[j, below], None if above is None else d_ref[j, above]),
            terms(fj_ref[j, i], own[j - 1] if j > 0 else None, own[j + 1] if j < nj - 1 else None),
        ]
        parts = [part for part in parts if part is not None]
        total = functools.reduce(jnp.add, [part[0] for part in parts])
        drift = functools.reduce(jnp.add, [part[1] for part in parts])
        o_ref[j, i] = (1.0 - 6.0 * RATE) * m + drift + RATE * total


def update_rows(d_ref, flow_refs, o_ref, start, stop):
    ni = d_ref.shape[1]
    if start == 0:
        update(d_ref, flow_refs, o_ref, 0, None, 1 if ni > 1 else None)
    lo, hi = max(start, 1), min(stop, ni - 1)
    if hi > lo:

        @pl.loop(lo, hi)
        def _(i):
            update(d_ref, flow_refs, o_ref, i, i - 1, i + 1)

    if stop == ni and ni > 1:
        update(d_ref, flow_refs, o_ref, ni - 1, ni - 2, None)


def main_kernel(d_ref, fj_ref, fi_ref, fk_ref, o_ref):
    update_rows(d_ref, (fj_ref, fi_ref, fk_ref), o_ref, 0, d_ref.shape[1])


def first_kernel(d_ref, fj_hbm, fi_hbm, fk_hbm, o_ref, fj_ref, fi_ref, fk_ref, sems):
    ni = d_ref.shape[1]
    pieces = sems.shape[1]
    rows = ni // pieces
    flow_refs = (fj_ref, fi_ref, fk_ref)

    def copy(n, piece):
        at = pl.ds(piece * rows, rows)
        hbm = (fj_hbm, fi_hbm, fk_hbm)[n]
        return pltpu.make_async_copy(hbm.at[:, at], flow_refs[n].at[:, at], sems.at[n, piece])

    for piece in range(pieces):
        for n in range(3):
            copy(n, piece).start()
    for piece in range(pieces):
        for n in range(3):
            copy(n, piece).wait()
        update_rows(d_ref, flow_refs, o_ref, piece * rows, (piece + 1) * rows)


def patch_kernel(counts, emit, *refs):
    d_ref, fj_ref, fi_ref, fk_ref = refs[:4]
    size = sum(len(rounds(count)) for count in counts)
    halos = grouped(refs[4 : 4 + size], counts)
    o_ref = refs[4 + size]
    nj, ni, nk, _ = d_ref.shape
    tile = 8
    row = lax.broadcasted_iota(jnp.int32, (tile, d_ref.shape[3]), 0)
    for (start, sign), halo in zip(sides(2, counts[2], nk, tile), halos[2]):
        start = pl.multiple_of(start, tile)
        mask = jnp.where(row == jnp.where(sign > 0, 0, tile - 1), 1.0, 0.0)
        for j in range(nj):

            @pl.loop(0, ni, unroll=8)
            def _(i, j=j, start=start, sign=sign, mask=mask, halo=halo):
                weight = (RATE + sign * fk_ref[j, i, pl.ds(start, tile)]) * mask
                o_ref[j, i, pl.ds(start, tile)] = d_ref[j, i, pl.ds(start, tile)] + weight * halo[j, pl.ds(i, 1)]

    for (at, sign), halo in zip(sides(1, counts[1], ni), halos[1]):
        for j in range(nj):
            o_ref[j, at] = o_ref[j, at] + (RATE + sign * fi_ref[j, at]) * halo[j]
    for (at, sign), halo in zip(sides(0, counts[0], nj), halos[0]):

        @pl.loop(0, ni, unroll=2)
        def _(i, at=at, sign=sign, halo=halo):
            o_ref[at, i] = o_ref[at, i] + (RATE + sign * fj_ref[at, i]) * halo[i]

    if emit:
        faces = grouped(refs[5 + size :], counts)
        copy_face_j(counts, o_ref, faces)
        copy_faces(counts, o_ref, faces)


VM = pl.BlockSpec(memory_space=pltpu.VMEM)
HBM = pl.BlockSpec(memory_space=pltpu.HBM)


def per_device(density, *flows):
    counts = [lax.axis_size(axis) for axis in AXES]
    shape, dtype = density.shape, density.dtype
    cells = density.size
    whole = pltpu.VMEM(shape, dtype)
    faces_out = [
        pltpu.VMEM(shape[:d] + shape[d + 1 :], dtype) for d in range(3) for _ in rounds(counts[d])
    ]
    params = pltpu.CompilerParams(vmem_limit_bytes=24 * 2**20)

    def cost(flops, moved):
        return pl.CostEstimate(flops=flops * cells, bytes_accessed=moved * cells, transcendentals=0)

    def patch(x, halos, emit):
        flat = [h for hs in halos for h in hs]
        outs = [whole] + (faces_out if emit else [])
        got = pl.pallas_call(
            functools.partial(patch_kernel, counts, emit),
            out_shape=outs,
            in_specs=[VM] * (4 + len(flat)),
            out_specs=[VM] * len(outs),
            input_output_aliases={0: 0},
            name="patch",
            compiler_params=params,
            cost_estimate=cost(1, 1),
        )(x, *flows, *flat)
        return got[0], list(got[1:])

    density, *faces = pl.pallas_call(
        functools.partial(load_kernel, counts),
        out_shape=[whole] + faces_out,
        in_specs=[HBM],
        out_specs=[VM] * (1 + len(faces_out)),
        scratch_shapes=[pltpu.SemaphoreType.DMA((shape[0],))],
        name="load",
        compiler_params=params,
        cost_estimate=cost(1, 4),
    )(density)
    for step in range(STEPS):
        groups = grouped(faces, counts)
        halos = [None] * 3
        for dim in (1, 0, 2):
            halos[dim] = exchange(AXES[dim], groups[dim])
        if step == 0:
            density, *flows = pl.pallas_call(
                first_kernel,
                out_shape=[whole] * 4,
                in_specs=[VM] + [HBM] * 3,
                out_specs=[VM] * 4,
                scratch_shapes=[pltpu.SemaphoreType.DMA((3, PIECES if shape[1] % PIECES == 0 else 1))],
                name="first",
                compiler_params=params,
                cost_estimate=cost(24, 20),
            )(density, *flows)
        else:
            density = pl.pallas_call(
                main_kernel,
                out_shape=whole,
                in_specs=[VM] * 4,
                out_specs=VM,
                name="main",
                compiler_params=params,
                cost_estimate=cost(24, 20),
            )(density, *flows)
        density, faces = patch(density, halos, step < STEPS - 1)
    return density


def solution(mesh):
    spec = P(("ens", "south"), "east", "down", None)
    return jax.shard_map(per_device, mesh=mesh, in_specs=(spec,) * 4, out_specs=spec, check_vma=False)
```

time: 119 us -> 37 us (0.31)
  waiting for transfers between devices: 37.1 us -> 1.63 us
  other arithmetic: 33.8 us -> 0 us
  starting transfers between devices: 42.3 us -> 15.3 us
  Pallas kernels: 0 us -> 13.3 us
  local copies, waits for them, and re-layouts: 4.86 us -> 6.39 us
    ppermute x18 -> x12, waiting for transfers between devices: 37.1 us -> 1.63 us  [exchange(): lax.ppermute(face, axis, up + [(j, i) for i, j in up])]
    add x3 -> x0, other arithmetic: 33.3 us -> none  [advance(): middle - flow_j * slopes[0] - flow_i * slopes[1] - flow_k * slopes[2]]
    ppermute x18 -> x12, starting transfers between devices: 42.3 us -> 15.3 us  [exchange(): lax.ppermute(face, axis, up + [(j, i) for i, j in up])]
    pallas_call x0 -> x7, Pallas kernels: none -> 13.3 us  [the longest x2 5.85 us: per_device(): pl.pallas_call(main_kernel, out_shape=whole, in_specs=[VM] * 4, out_specs...]
    unnamed x12 -> x7, local copies, waits for them, and re-layouts: 0.67 us -> 6.39 us
    slice x10 -> x0, local copies, waits for them, and re-layouts: 2.19 us -> none  [the longest x4 1.86 us: padded_2(): initial = lax.slice_in_dim(x, 0, width, axis=dim)]
    ppermute x6 -> x0, local copies, waits for them, and re-layouts: 1.93 us -> none  [the longest x3 0.97 us: padded_2(): before = lax.ppermute(last, axis, up)]
  transfers between devices with their start and end apart: 18 -> 12, of which waited for: 18 -> 2; matrix products, arithmetic and copies ran while one was open for 1% -> 0% of each run, Pallas kernels for 0% -> 28%
where the time goes in v2:
time: 37 us; the launch traced here: 36.8 us
  starting transfers between devices  15.3 us (41%)
  Pallas kernels  13.3 us (36%)
  local copies, waits for them, and re-layouts  6.39 us (17%)
  waiting for transfers between devices  1.63 us (4%)
    ppermute x12, starting transfers between devices, exchange(): lax.ppermute(face, axis, up + [(j, i) for i, j in up])  15.3 us
    unnamed x7, local copies, waits for them, and re-layouts  6.39 us
    pallas_call x2, Pallas kernels, per_device(): pl.pallas_call(main_kernel, out_shape=whole, in_specs=[VM] * 4, out_specs...  5.85 us
    pallas_call x1, Pallas kernels, per_device(): pl.pallas_call(first_kernel, out_shape=[whole] * 4, in_specs=[VM] + [HBM]...  4.27 us
    pallas_call x3, Pallas kernels, patch(): pl.pallas_call(functools.partial(patch_kernel, counts, emit), out_shape=o...  2.63 us
    ppermute x12, waiting for transfers between devices, exchange(): lax.ppermute(face, axis, up + [(j, i) for i, j in up])  1.63 us
  transfers between devices with their start and end apart: 12, of which 2 were waited for; matrix products, arithmetic and copies ran while one was open for 0% of the time, Pallas kernels for 28%

profile of v2, /device:TPU:0, one launch (start us, length us, event | category | flops | bytes accessed | tf_op | source)
XLA Modules:
  0.0 36.8 jit_solution(3877121413933949722)
XLA Ops:
  0.0 2.2 %copy-done = f32[4,32,64,128]{3,2,1,0:T(8,128)S(1)} copy-done((f32[4,32,64,128]{3,2,1,0:T(8,128)S(1)}, f32[4,32,64,128]{3,2,1,0:T(8,128)}, u32[]{:S(2)}) %copy-start) | copy-done | bytes 4194328
  2.2 0.6 %load.1 = (f32[4,32,64,128]{3,2,1,0:T(8,128)S(1)}, f32[32,64,128]{2,1,0:T(8,128)S(1)}, f32[4,64,128]{2,1,0:T(8,128)S(1)}, f32[4,64,128]{2,1,0:T(8,128)S(1)}, f32[4,32,128]{2,1,0:T(8,128)S(1)}) custom-call(f32[4,32,64,128]{3,2,1,0:T(8,128)S(1)} %copy-done), custom_call_target="tpu_custom_call" | custom-call | flops 1048576 | bytes 4194304 | tf_op jit(solution)/shard_map/load/pallas_call | solution.py:211
  2.8 0.6 %collective-permute-start = (f32[32,64,128]{2,1,0:T(8,128)S(1)}, f32[32,64,128]{2,1,0:T(8,128)S(1)}, u32[]{:S(2)}, u32[]{:S(2)}) collective-permute-start(f32[32,64,128]{2,1,0:T(8,128)S(1)} %get-tuple-element.29), channel_id=1, source_target_pairs={{0,16},{16,0},{1,17},{17,1},{2,18},{18,2},{3,19},{19,3},{4,20},{20... | collective-permute-start | bytes 3145736 | tf_op jit(solution)/shard_map/ppermute | solution.py:22
  3.3 2.6 %collective-permute-start.1 = (f32[4,64,128]{2,1,0:T(8,128)S(1)}, f32[4,64,128]{2,1,0:T(8,128)S(1)}, u32[]{:S(2)}, u32[]{:S(2)}) collective-permute-start(f32[4,64,128]{2,1,0:T(8,128)S(1)} %get-tuple-element.30), channel_id=1, source_target_pairs={{0,4},{8,12},{4,0},{12,8},{1,5},{9,13},{5,1},{13,9},{2,6},{10,14},... | collective-permute-start | bytes 393224 | tf_op jit(solution)/shard_map/ppermute | solution.py:22
  6.0 0.7 %collective-permute-start.2 = (f32[4,64,128]{2,1,0:T(8,128)S(1)}, f32[4,64,128]{2,1,0:T(8,128)S(1)}, u32[]{:S(2)}, u32[]{:S(2)}) collective-permute-start(f32[4,64,128]{2,1,0:T(8,128)S(1)} %get-tuple-element.31), channel_id=1, source_target_pairs={{4,8},{8,4},{5,9},{9,5},{6,10},{10,6},{7,11},{11,7},{20,24},{24,20... | collective-permute-start | bytes 393224 | tf_op jit(solution)/shard_map/ppermute | solution.py:22
  6.6 1.6 %collective-permute-start.3 = (f32[4,32,128]{2,1,0:T(8,128)S(1)}, f32[4,32,128]{2,1,0:T(8,128)S(1)}, u32[]{:S(2)}, u32[]{:S(2)}) collective-permute-start(f32[4,32,128]{2,1,0:T(8,128)S(1)} %get-tuple-element.32), channel_id=1, source_target_pairs={{0,2},{2,0},{1,3},{3,1},{4,6},{6,4},{5,7},{7,5},{8,10},{10,8},{9,1... | collective-permute-start | bytes 196616 | tf_op jit(solution)/shard_map/ppermute | solution.py:22
  8.2 2.2 %copy-done.2 = f32[4,32,64,128]{3,2,1,0:T(8,128)S(1)} copy-done((f32[4,32,64,128]{3,2,1,0:T(8,128)S(1)}, f32[4,32,64,128]{3,2,1,0:T(8,128)}, u32[]{:S(2)}) %copy-start.2) | copy-done | bytes 4194328
  10.4 4.3 %first.1 = (f32[4,32,64,128]{3,2,1,0:T(8,128)S(1)}, f32[4,32,64,128]{3,2,1,0:T(8,128)S(1)}, f32[4,32,64,128]{3,2,1,0:T(8,128)S(1)}, f32[4,32,64,128]{3,2,1,0:T(8,128)S(1)}) custom-call(f32[4,32,64,128]{3,2,1,0:T(8,128)S(1)} %get-tuple-element.24.d_ref, f32[4,32,64,128]{3,2,1,0:T(8,128)S(1)} %copy-done.1, f32[4,32,64,128]{3,2,1,0:T(8,128)S(1)} %copy-done.2, ...), custom_call_target="tpu_custom_call" | custom-call | flops 25165824 | bytes 20971520 | tf_op jit(solution)/shard_map/first/pallas_call | solution.py:227
  14.7 0.0 collective-permute-done.3.refs_7_
  14.7 0.0 collective-permute-done.1.refs_5_
  14.7 0.0 collective-permute-done.2.refs_6_
  14.7 0.0 collective-permute-done.refs_4_
  14.7 1.0 %patch.3 = (f32[4,32,64,128]{3,2,1,0:T(8,128)S(1)}, f32[32,64,128]{2,1,0:T(8,128)S(1)}, f32[4,64,128]{2,1,0:T(8,128)S(1)}, f32[4,64,128]{2,1,0:T(8,128)S(1)}, f32[4,32,128]{2,1,0:T(8,128)S(1)}) custom-call(f32[4,32,64,128]{3,2,1,0:T(8,128)S(1)} %get-tuple-element.25.refs_0_, ...), custom_call_target="tpu_custom_call", output_to_operand_aliasing={{0}: (0, {})} | custom-call | flops 1048576 | bytes 1048576 | tf_op jit(solution)/shard_map/patch/pallas_call | solution.py:199
  15.7 0.1 collective-permute-start.4
  15.8 4.5 %collective-permute-start.5 = (f32[4,64,128]{2,1,0:T(8,128)S(1)}, f32[4,64,128]{2,1,0:T(8,128)S(1)}, u32[]{:S(2)}, u32[]{:S(2)}) collective-permute-start(f32[4,64,128]{2,1,0:T(8,128)S(1)} %get-tuple-element.35), channel_id=1, source_target_pairs={{0,4},{8,12},{4,0},{12,8},{1,5},{9,13},{5,1},{13,9},{2,6},{10,14},... | collective-permute-start | bytes 393224 | tf_op jit(solution)/shard_map/ppermute | solution.py:22
  20.2 0.7 %collective-permute-start.6 = (f32[4,64,128]{2,1,0:T(8,128)S(1)}, f32[4,64,128]{2,1,0:T(8,128)S(1)}, u32[]{:S(2)}, u32[]{:S(2)}) collective-permute-start(f32[4,64,128]{2,1,0:T(8,128)S(1)} %get-tuple-element.36), channel_id=1, source_target_pairs={{4,8},{8,4},{5,9},{9,5},{6,10},{10,6},{7,11},{11,7},{20,24},{24,20... | collective-permute-start | bytes 393224 | tf_op jit(solution)/shard_map/ppermute | solution.py:22
  20.9 0.6 %collective-permute-start.7 = (f32[4,32,128]{2,1,0:T(8,128)S(1)}, f32[4,32,128]{2,1,0:T(8,128)S(1)}, u32[]{:S(2)}, u32[]{:S(2)}) collective-permute-start(f32[4,32,128]{2,1,0:T(8,128)S(1)} %get-tuple-element.37), channel_id=1, source_target_pairs={{0,2},{2,0},{1,3},{3,1},{4,6},{6,4},{5,7},{7,5},{8,10},{10,8},{9,1... | collective-permute-start | bytes 196616 | tf_op jit(solution)/shard_map/ppermute | solution.py:22
  21.5 2.9 %main.2.refs_0_ = f32[4,32,64,128]{3,2,1,0:T(8,128)S(1)} custom-call(f32[4,32,64,128]{3,2,1,0:T(8,128)S(1)} %get-tuple-element.33.d_ref, f32[4,32,64,128]{3,2,1,0:T(8,128)S(1)} %get-tuple-element.26.refs_1_.fj_ref, f32[4,32,64,128]{3,2,1,0:T(8,128)S(1)} %get-tuple-element.27.refs_2_.fi_ref, f32[4,32,64,128]{3,2,1,0:T(8,128)S(1)} %get-tuple-element.28.refs_3_.fk_ref), custom_call_target="tpu_custom_call" | custom-call | flops 25165824 | bytes 20971520 | tf_op jit(solution)/shard_map/main/pallas_call | solution.py:238
  24.4 0.8 %collective-permute-done.7.refs_7_ = f32[4,32,128]{2,1,0:T(8,128)S(1)} collective-permute-done((f32[4,32,128]{2,1,0:T(8,128)S(1)}, f32[4,32,128]{2,1,0:T(8,128)S(1)}, u32[]{:S(2)}, u32[]{:S(2)}) %collective-permute-start.7) | collective-permute-done | bytes 65568 | tf_op jit(solution)/shard_map/ppermute | solution.py:22
  25.2 0.0 collective-permute-done.5.refs_5_
  25.2 1.0 %patch.4 = (f32[4,32,64,128]{3,2,1,0:T(8,128)S(1)}, f32[32,64,128]{2,1,0:T(8,128)S(1)}, f32[4,64,128]{2,1,0:T(8,128)S(1)}, f32[4,64,128]{2,1,0:T(8,128)S(1)}, f32[4,32,128]{2,1,0:T(8,128)S(1)}) custom-call(f32[4,32,64,128]{3,2,1,0:T(8,128)S(1)} %main.2.refs_0_, ...), custom_call_target="tpu_custom_call", output_to_operand_aliasing={{0}: (0, {})} | custom-call | flops 1048576 | bytes 1048576 | tf_op jit(solution)/shard_map/patch/pallas_call | solution.py:199
  26.2 0.1 collective-permute-start.8
  26.3 2.8 %collective-permute-start.9 = (f32[4,64,128]{2,1,0:T(8,128)S(1)}, f32[4,64,128]{2,1,0:T(8,128)S(1)}, u32[]{:S(2)}, u32[]{:S(2)}) collective-permute-start(f32[4,64,128]{2,1,0:T(8,128)S(1)} %get-tuple-element.40), channel_id=1, source_target_pairs={{0,4},{8,12},{4,0},{12,8},{1,5},{9,13},{5,1},{13,9},{2,6},{10,14},... | collective-permute-start | bytes 393224 | tf_op jit(solution)/shard_map/ppermute | solution.py:22
  29.0 0.7 %collective-permute-start.10 = (f32[4,64,128]{2,1,0:T(8,128)S(1)}, f32[4,64,128]{2,1,0:T(8,128)S(1)}, u32[]{:S(2)}, u32[]{:S(2)}) collective-permute-start(f32[4,64,128]{2,1,0:T(8,128)S(1)} %get-tuple-element.41), channel_id=1, source_target_pairs={{4,8},{8,4},{5,9},{9,5},{6,10},{10,6},{7,11},{11,7},{20,24},{24,20... | collective-permute-start | bytes 393224 | tf_op jit(solution)/shard_map/ppermute | solution.py:22
  29.7 0.6 %collective-permute-start.11 = (f32[4,32,128]{2,1,0:T(8,128)S(1)}, f32[4,32,128]{2,1,0:T(8,128)S(1)}, u32[]{:S(2)}, u32[]{:S(2)}) collective-permute-start(f32[4,32,128]{2,1,0:T(8,128)S(1)} %get-tuple-element.42), channel_id=1, source_target_pairs={{0,2},{2,0},{1,3},{3,1},{4,6},{6,4},{5,7},{7,5},{8,10},{10,8},{9,1... | collective-permute-start | bytes 196616 | tf_op jit(solution)/shard_map/ppermute | solution.py:22
  30.3 2.9 %main.3.refs_0_ = f32[4,32,64,128]{3,2,1,0:T(8,128)S(1)} custom-call(f32[4,32,64,128]{3,2,1,0:T(8,128)S(1)} %get-tuple-element.38.d_ref, f32[4,32,64,128]{3,2,1,0:T(8,128)S(1)} %get-tuple-element.26.refs_1_.fj_ref, f32[4,32,64,128]{3,2,1,0:T(8,128)S(1)} %get-tuple-element.27.refs_2_.fi_ref, f32[4,32,64,128]{3,2,1,0:T(8,128)S(1)} %get-tuple-element.28.refs_3_.fk_ref), custom_call_target="tpu_custom_call" | custom-call | flops 25165824 | bytes 20971520 | tf_op jit(solution)/shard_map/main/pallas_call | solution.py:238
  33.2 0.8 %collective-permute-done.11.refs_7_ = f32[4,32,128]{2,1,0:T(8,128)S(1)} collective-permute-done((f32[4,32,128]{2,1,0:T(8,128)S(1)}, f32[4,32,128]{2,1,0:T(8,128)S(1)}, u32[]{:S(2)}, u32[]{:S(2)}) %collective-permute-start.11) | collective-permute-done | bytes 65568 | tf_op jit(solution)/shard_map/ppermute | solution.py:22
  34.0 0.0 collective-permute-done.9.refs_5_
  34.0 0.0 collective-permute-done.10.refs_6_
  34.0 0.0 collective-permute-done.8.refs_4_
  34.0 0.7 %patch.5 = f32[4,32,64,128]{3,2,1,0:T(8,128)S(1)} custom-call(f32[4,32,64,128]{3,2,1,0:T(8,128)S(1)} %main.3.refs_0_, f32[4,32,64,128]{3,2,1,0:T(8,128)S(1)} %get-tuple-element.26.refs_1_.fj_ref, f32[4,32,64,128]{3,2,1,0:T(8,128)S(1)} %get-tuple-element.27.refs_2_.fi_ref, ...), custom_call_target="tpu_custom_call", output_to_operand_aliasing={{}: (0, {})} | custom-call | flops 1048576 | bytes 1048576 | tf_op jit(solution)/shard_map/patch/pallas_call | solution.py:199
  34.8 2.0 %copy.11 = f32[4,32,64,128]{3,2,1,0:T(8,128)} copy(f32[4,32,64,128]{3,2,1,0:T(8,128)S(1)} %patch.5) | data formatting | bytes 8388608
  (6 shorter events, 0.0 us)
Async XLA Ops:
  0.0 2.2 %copy-start = (f32[4,32,64,128]{3,2,1,0:T(8,128)S(1)}, f32[4,32,64,128]{3,2,1,0:T(8,128)}, u32[]{:S(2)}) copy-start(f32[4,32,64,128]{3,2,1,0:T(8,128)} %x_ref.1) | copy-start | bytes 12582916
  2.2 6.0 %copy-start.1 = (f32[4,32,64,128]{3,2,1,0:T(8,128)S(1)}, f32[4,32,64,128]{3,2,1,0:T(8,128)}, u32[]{:S(2)}) copy-start(f32[4,32,64,128]{3,2,1,0:T(8,128)} %fj_hbm.1) | copy-start | bytes 12582916
  2.8 11.9 %collective-permute-start = (f32[32,64,128]{2,1,0:T(8,128)S(1)}, f32[32,64,128]{2,1,0:T(8,128)S(1)}, u32[]{:S(2)}, u32[]{:S(2)}) collective-permute-start(f32[32,64,128]{2,1,0:T(8,128)S(1)} %get-tuple-element.29), channel_id=1, source_target_pairs={{0,16},{16,0},{1,17},{17,1},{2,18},{18,2},{3,19},{19,3},{4,20},{20... | collective-permute-start | bytes 3145736 | tf_op jit(solution)/shard_map/ppermute | solution.py:22
  3.3 11.3 %collective-permute-start.1 = (f32[4,64,128]{2,1,0:T(8,128)S(1)}, f32[4,64,128]{2,1,0:T(8,128)S(1)}, u32[]{:S(2)}, u32[]{:S(2)}) collective-permute-start(f32[4,64,128]{2,1,0:T(8,128)S(1)} %get-tuple-element.30), channel_id=1, source_target_pairs={{0,4},{8,12},{4,0},{12,8},{1,5},{9,13},{5,1},{13,9},{2,6},{10,14},... | collective-permute-start | bytes 393224 | tf_op jit(solution)/shard_map/ppermute | solution.py:22
  6.0 8.7 %collective-permute-start.2 = (f32[4,64,128]{2,1,0:T(8,128)S(1)}, f32[4,64,128]{2,1,0:T(8,128)S(1)}, u32[]{:S(2)}, u32[]{:S(2)}) collective-permute-start(f32[4,64,128]{2,1,0:T(8,128)S(1)} %get-tuple-element.31), channel_id=1, source_target_pairs={{4,8},{8,4},{5,9},{9,5},{6,10},{10,6},{7,11},{11,7},{20,24},{24,20... | collective-permute-start | bytes 393224 | tf_op jit(solution)/shard_map/ppermute | solution.py:22
  6.6 8.0 %collective-permute-start.3 = (f32[4,32,128]{2,1,0:T(8,128)S(1)}, f32[4,32,128]{2,1,0:T(8,128)S(1)}, u32[]{:S(2)}, u32[]{:S(2)}) collective-permute-start(f32[4,32,128]{2,1,0:T(8,128)S(1)} %get-tuple-element.32), channel_id=1, source_target_pairs={{0,2},{2,0},{1,3},{3,1},{4,6},{6,4},{5,7},{7,5},{8,10},{10,8},{9,1... | collective-permute-start | bytes 196616 | tf_op jit(solution)/shard_map/ppermute | solution.py:22
  8.2 2.2 %copy-start.2 = (f32[4,32,64,128]{3,2,1,0:T(8,128)S(1)}, f32[4,32,64,128]{3,2,1,0:T(8,128)}, u32[]{:S(2)}) copy-start(f32[4,32,64,128]{3,2,1,0:T(8,128)} %fi_hbm.1) | copy-start | bytes 12582916
  15.7 9.5 %collective-permute-start.4 = (f32[32,64,128]{2,1,0:T(8,128)S(1)}, f32[32,64,128]{2,1,0:T(8,128)S(1)}, u32[]{:S(2)}, u32[]{:S(2)}) collective-permute-start(f32[32,64,128]{2,1,0:T(8,128)S(1)} %get-tuple-element.34), channel_id=1, source_target_pairs={{0,16},{16,0},{1,17},{17,1},{2,18},{18,2},{3,19},{19,3},{4,20},{20... | collective-permute-start | bytes 3145736 | tf_op jit(solution)/shard_map/ppermute | solution.py:22
  15.8 9.5 %collective-permute-start.5 = (f32[4,64,128]{2,1,0:T(8,128)S(1)}, f32[4,64,128]{2,1,0:T(8,128)S(1)}, u32[]{:S(2)}, u32[]{:S(2)}) collective-permute-start(f32[4,64,128]{2,1,0:T(8,128)S(1)} %get-tuple-element.35), channel_id=1, source_target_pairs={{0,4},{8,12},{4,0},{12,8},{1,5},{9,13},{5,1},{13,9},{2,6},{10,14},... | collective-permute-start | bytes 393224 | tf_op jit(solution)/shard_map/ppermute | solution.py:22
  20.2 5.0 %collective-permute-start.6 = (f32[4,64,128]{2,1,0:T(8,128)S(1)}, f32[4,64,128]{2,1,0:T(8,128)S(1)}, u32[]{:S(2)}, u32[]{:S(2)}) collective-permute-start(f32[4,64,128]{2,1,0:T(8,128)S(1)} %get-tuple-element.36), channel_id=1, source_target_pairs={{4,8},{8,4},{5,9},{9,5},{6,10},{10,6},{7,11},{11,7},{20,24},{24,20... | collective-permute-start | bytes 393224 | tf_op jit(solution)/shard_map/ppermute | solution.py:22
  20.9 4.3 %collective-permute-start.7 = (f32[4,32,128]{2,1,0:T(8,128)S(1)}, f32[4,32,128]{2,1,0:T(8,128)S(1)}, u32[]{:S(2)}, u32[]{:S(2)}) collective-permute-start(f32[4,32,128]{2,1,0:T(8,128)S(1)} %get-tuple-element.37), channel_id=1, source_target_pairs={{0,2},{2,0},{1,3},{3,1},{4,6},{6,4},{5,7},{7,5},{8,10},{10,8},{9,1... | collective-permute-start | bytes 196616 | tf_op jit(solution)/shard_map/ppermute | solution.py:22
  26.2 7.8 %collective-permute-start.8 = (f32[32,64,128]{2,1,0:T(8,128)S(1)}, f32[32,64,128]{2,1,0:T(8,128)S(1)}, u32[]{:S(2)}, u32[]{:S(2)}) collective-permute-start(f32[32,64,128]{2,1,0:T(8,128)S(1)} %get-tuple-element.39), channel_id=1, source_target_pairs={{0,16},{16,0},{1,17},{17,1},{2,18},{18,2},{3,19},{19,3},{4,20},{20... | collective-permute-start | bytes 3145736 | tf_op jit(solution)/shard_map/ppermute | solution.py:22
  26.3 7.8 %collective-permute-start.9 = (f32[4,64,128]{2,1,0:T(8,128)S(1)}, f32[4,64,128]{2,1,0:T(8,128)S(1)}, u32[]{:S(2)}, u32[]{:S(2)}) collective-permute-start(f32[4,64,128]{2,1,0:T(8,128)S(1)} %get-tuple-element.40), channel_id=1, source_target_pairs={{0,4},{8,12},{4,0},{12,8},{1,5},{9,13},{5,1},{13,9},{2,6},{10,14},... | collective-permute-start | bytes 393224 | tf_op jit(solution)/shard_map/ppermute | solution.py:22
  29.0 5.0 %collective-permute-start.10 = (f32[4,64,128]{2,1,0:T(8,128)S(1)}, f32[4,64,128]{2,1,0:T(8,128)S(1)}, u32[]{:S(2)}, u32[]{:S(2)}) collective-permute-start(f32[4,64,128]{2,1,0:T(8,128)S(1)} %get-tuple-element.41), channel_id=1, source_target_pairs={{4,8},{8,4},{5,9},{9,5},{6,10},{10,6},{7,11},{11,7},{20,24},{24,20... | collective-permute-start | bytes 393224 | tf_op jit(solution)/shard_map/ppermute | solution.py:22
  29.7 4.3 %collective-permute-start.11 = (f32[4,32,128]{2,1,0:T(8,128)S(1)}, f32[4,32,128]{2,1,0:T(8,128)S(1)}, u32[]{:S(2)}, u32[]{:S(2)}) collective-permute-start(f32[4,32,128]{2,1,0:T(8,128)S(1)} %get-tuple-element.42), channel_id=1, source_target_pairs={{0,2},{2,0},{1,3},{3,1},{4,6},{6,4},{5,7},{7,5},{8,10},{10,8},{9,1... | collective-permute-start | bytes 196616 | tf_op jit(solution)/shard_map/ppermute | solution.py:22

commit v3 on v2

--- a/solution.py
+++ b/solution.py
@@ -7,19 +7,24 @@
 from jax.experimental.pallas import tpu as pltpu
 from jax.sharding import PartitionSpec as P
 
+
 STEPS = 3
 AXES = ("south", "east", "down")
 RATE = 0.05
 PIECES = 8
+ORDER = (1, 0, 2)
 
 
 def rounds(count):
     return [[(i, i + 1) for i in range(begin, count - 1, 2)] for begin in range(min(2, count - 1))]
 
 
-def exchange(axis, faces):
-    pairs = rounds(lax.axis_size(axis))
-    return [lax.ppermute(face, axis, up + [(j, i) for i, j in up]) for face, up in zip(faces, pairs)]
+def exchange_all(groups, counts):
+    halos = [[] for _ in AXES]
+    for dim in ORDER:
+        for face, up in zip(groups[dim], rounds(counts[dim])):
+            halos[dim].append(lax.ppermute(face, AXES[dim], up + [(j, i) for i, j in up]))
+    return halos
 
 
 def sides(dim, count, length, step=1):
@@ -119,8 +124,8 @@
         update(d_ref, flow_refs, o_ref, ni - 1, ni - 2, None)
 
 
-def main_kernel(d_ref, fj_ref, fi_ref, fk_ref, o_ref):
-    update_rows(d_ref, (fj_ref, fi_ref, fk_ref), o_ref, 0, d_ref.shape[1])
+def main_kernel(start, stop, d_ref, fj_ref, fi_ref, fk_ref, *refs):
+    update_rows(d_ref, (fj_ref, fi_ref, fk_ref), refs[-1], start, stop)
 
 
 def first_kernel(d_ref, fj_hbm, fi_hbm, fk_hbm, o_ref, fj_ref, fi_ref, fk_ref, sems):
@@ -218,11 +223,9 @@
         compiler_params=params,
         cost_estimate=cost(1, 4),
     )(density)
+    messages = len(faces_out)
     for step in range(STEPS):
-        groups = grouped(faces, counts)
-        halos = [None] * 3
-        for dim in (1, 0, 2):
-            halos[dim] = exchange(AXES[dim], groups[dim])
+        halos = exchange_all(grouped(faces, counts), counts)
         if step == 0:
             density, *flows = pl.pallas_call(
                 first_kernel,
@@ -235,15 +238,23 @@
                 cost_estimate=cost(24, 20),
             )(density, *flows)
         else:
-            density = pl.pallas_call(
-                main_kernel,
-                out_shape=whole,
-                in_specs=[VM] * 4,
-                out_specs=VM,
-                name="main",
-                compiler_params=params,
-                cost_estimate=cost(24, 20),
-            )(density, *flows)
+            parts = max(1, min(messages, shape[1]))
+            done = []
+            for part in range(parts):
+                start, stop = (shape[1] * at // parts for at in (part, part + 1))
+                done = [
+                    pl.pallas_call(
+                        functools.partial(main_kernel, start, stop),
+                        out_shape=whole,
+                        in_specs=[VM] * (4 + len(done)),
+                        out_specs=VM,
+                        input_output_aliases={4: 0} if done else {},
+                        name="main",
+                        compiler_params=params,
+                        cost_estimate=cost(24 // parts, 20 // parts),
+                    )(density, *flows, *done)
+                ]
+            density = done[0]
         density, faces = patch(density, halos, step < STEPS - 1)
     return density
 

time: 37 us -> 37 us (level)
    pallas_call x2 -> x8, Pallas kernels: 5.85 us -> 5.87 us  [per_device(): pl.pallas_call(functools.partial(main_kernel, start, stop), out_shape=who...]
where the time goes in v3:
time: 37 us; the launch traced here: 36.8 us
  starting transfers between devices  15.3 us (41%)
  Pallas kernels  13.3 us (36%)
  local copies, waits for them, and re-layouts  6.39 us (17%)
  waiting for transfers between devices  1.56 us (4%)
    ppermute x12, starting transfers between devices, exchange_all(): lax.ppermute(face, AXES[dim], up + [(j, i) for i, j in up])  15.3 us
    unnamed x7, local copies, waits for them, and re-layouts  6.39 us
    pallas_call x8, Pallas kernels, per_device(): pl.pallas_call(functools.partial(main_kernel, start, stop), out_shape=who...  5.87 us
    pallas_call x1, Pallas kernels, per_device(): pl.pallas_call(first_kernel, out_shape=[whole] * 4, in_specs=[VM] + [HBM]...  4.27 us
    pallas_call x3, Pallas kernels, patch(): pl.pallas_call(functools.partial(patch_kernel, counts, emit), out_shape=o...  2.63 us
    ppermute x12, waiting for transfers between devices, exchange_all(): lax.ppermute(face, AXES[dim], up + [(j, i) for i, j in up])  1.56 us
  transfers between devices with their start and end apart: 12, of which 2 were waited for; matrix products, arithmetic and copies ran while one was open for 0% of the time, Pallas kernels for 28%

profile of v3, /device:TPU:0, one launch (start us, length us, event | category | flops | bytes accessed | tf_op | source)
XLA Modules:
  0.0 36.8 jit_solution(10966858233887592420)
XLA Ops:
  0.0 2.2 %copy-done = f32[4,32,64,128]{3,2,1,0:T(8,128)S(1)} copy-done((f32[4,32,64,128]{3,2,1,0:T(8,128)S(1)}, f32[4,32,64,128]{3,2,1,0:T(8,128)}, u32[]{:S(2)}) %copy-start) | copy-done | bytes 4194328
  2.2 0.6 %load.1 = (f32[4,32,64,128]{3,2,1,0:T(8,128)S(1)}, f32[32,64,128]{2,1,0:T(8,128)S(1)}, f32[4,64,128]{2,1,0:T(8,128)S(1)}, f32[4,64,128]{2,1,0:T(8,128)S(1)}, f32[4,32,128]{2,1,0:T(8,128)S(1)}) custom-call(f32[4,32,64,128]{3,2,1,0:T(8,128)S(1)} %copy-done), custom_call_target="tpu_custom_call" | custom-call | flops 1048576 | bytes 4194304 | tf_op jit(solution)/shard_map/load/pallas_call | solution.py:216
  2.8 0.6 %collective-permute-start = (f32[32,64,128]{2,1,0:T(8,128)S(1)}, f32[32,64,128]{2,1,0:T(8,128)S(1)}, u32[]{:S(2)}, u32[]{:S(2)}) collective-permute-start(f32[32,64,128]{2,1,0:T(8,128)S(1)} %get-tuple-element.29), channel_id=1, source_target_pairs={{0,16},{16,0},{1,17},{17,1},{2,18},{18,2},{3,19},{19,3},{4,20},{20... | collective-permute-start | bytes 3145736 | tf_op jit(solution)/shard_map/ppermute | solution.py:26
  3.3 2.6 %collective-permute-start.1 = (f32[4,64,128]{2,1,0:T(8,128)S(1)}, f32[4,64,128]{2,1,0:T(8,128)S(1)}, u32[]{:S(2)}, u32[]{:S(2)}) collective-permute-start(f32[4,64,128]{2,1,0:T(8,128)S(1)} %get-tuple-element.30), channel_id=1, source_target_pairs={{0,4},{8,12},{4,0},{12,8},{1,5},{9,13},{5,1},{13,9},{2,6},{10,14},... | collective-permute-start | bytes 393224 | tf_op jit(solution)/shard_map/ppermute | solution.py:26
  6.0 0.7 %collective-permute-start.2 = (f32[4,64,128]{2,1,0:T(8,128)S(1)}, f32[4,64,128]{2,1,0:T(8,128)S(1)}, u32[]{:S(2)}, u32[]{:S(2)}) collective-permute-start(f32[4,64,128]{2,1,0:T(8,128)S(1)} %get-tuple-element.31), channel_id=1, source_target_pairs={{4,8},{8,4},{5,9},{9,5},{6,10},{10,6},{7,11},{11,7},{20,24},{24,20... | collective-permute-start | bytes 393224 | tf_op jit(solution)/shard_map/ppermute | solution.py:26
  6.6 1.6 %collective-permute-start.3 = (f32[4,32,128]{2,1,0:T(8,128)S(1)}, f32[4,32,128]{2,1,0:T(8,128)S(1)}, u32[]{:S(2)}, u32[]{:S(2)}) collective-permute-start(f32[4,32,128]{2,1,0:T(8,128)S(1)} %get-tuple-element.32), channel_id=1, source_target_pairs={{0,2},{2,0},{1,3},{3,1},{4,6},{6,4},{5,7},{7,5},{8,10},{10,8},{9,1... | collective-permute-start | bytes 196616 | tf_op jit(solution)/shard_map/ppermute | solution.py:26
  8.2 2.2 %copy-done.2 = f32[4,32,64,128]{3,2,1,0:T(8,128)S(1)} copy-done((f32[4,32,64,128]{3,2,1,0:T(8,128)S(1)}, f32[4,32,64,128]{3,2,1,0:T(8,128)}, u32[]{:S(2)}) %copy-start.2) | copy-done | bytes 4194328
  10.4 4.3 %first.1 = (f32[4,32,64,128]{3,2,1,0:T(8,128)S(1)}, f32[4,32,64,128]{3,2,1,0:T(8,128)S(1)}, f32[4,32,64,128]{3,2,1,0:T(8,128)S(1)}, f32[4,32,64,128]{3,2,1,0:T(8,128)S(1)}) custom-call(f32[4,32,64,128]{3,2,1,0:T(8,128)S(1)} %get-tuple-element.24.d_ref, f32[4,32,64,128]{3,2,1,0:T(8,128)S(1)} %copy-done.1, f32[4,32,64,128]{3,2,1,0:T(8,128)S(1)} %copy-done.2, ...), custom_call_target="tpu_custom_call" | custom-call | flops 25165824 | bytes 20971520 | tf_op jit(solution)/shard_map/first/pallas_call | solution.py:230
  14.7 0.0 collective-permute-done.1.refs_5_
  14.7 0.0 collective-permute-done.2.refs_6_
  14.7 1.0 %patch.3 = (f32[4,32,64,128]{3,2,1,0:T(8,128)S(1)}, f32[32,64,128]{2,1,0:T(8,128)S(1)}, f32[4,64,128]{2,1,0:T(8,128)S(1)}, f32[4,64,128]{2,1,0:T(8,128)S(1)}, f32[4,32,128]{2,1,0:T(8,128)S(1)}) custom-call(f32[4,32,64,128]{3,2,1,0:T(8,128)S(1)} %get-tuple-element.25.refs_0_, ...), custom_call_target="tpu_custom_call", output_to_operand_aliasing={{0}: (0, {})} | custom-call | flops 1048576 | bytes 1048576 | tf_op jit(solution)/shard_map/patch/pallas_call | solution.py:204
  15.7 0.1 collective-permute-start.4
  15.8 4.5 %collective-permute-start.5 = (f32[4,64,128]{2,1,0:T(8,128)S(1)}, f32[4,64,128]{2,1,0:T(8,128)S(1)}, u32[]{:S(2)}, u32[]{:S(2)}) collective-permute-start(f32[4,64,128]{2,1,0:T(8,128)S(1)} %get-tuple-element.35), channel_id=1, source_target_pairs={{0,4},{8,12},{4,0},{12,8},{1,5},{9,13},{5,1},{13,9},{2,6},{10,14},... | collective-permute-start | bytes 393224 | tf_op jit(solution)/shard_map/ppermute | solution.py:26
  20.2 0.7 %collective-permute-start.6 = (f32[4,64,128]{2,1,0:T(8,128)S(1)}, f32[4,64,128]{2,1,0:T(8,128)S(1)}, u32[]{:S(2)}, u32[]{:S(2)}) collective-permute-start(f32[4,64,128]{2,1,0:T(8,128)S(1)} %get-tuple-element.36), channel_id=1, source_target_pairs={{4,8},{8,4},{5,9},{9,5},{6,10},{10,6},{7,11},{11,7},{20,24},{24,20... | collective-permute-start | bytes 393224 | tf_op jit(solution)/shard_map/ppermute | solution.py:26
  20.9 0.6 %collective-permute-start.7 = (f32[4,32,128]{2,1,0:T(8,128)S(1)}, f32[4,32,128]{2,1,0:T(8,128)S(1)}, u32[]{:S(2)}, u32[]{:S(2)}) collective-permute-start(f32[4,32,128]{2,1,0:T(8,128)S(1)} %get-tuple-element.37), channel_id=1, source_target_pairs={{0,2},{2,0},{1,3},{3,1},{4,6},{6,4},{5,7},{7,5},{8,10},{10,8},{9,1... | collective-permute-start | bytes 196616 | tf_op jit(solution)/shard_map/ppermute | solution.py:26
  21.5 0.7 %main.8.refs_0_ = f32[4,32,64,128]{3,2,1,0:T(8,128)S(1)} custom-call(f32[4,32,64,128]{3,2,1,0:T(8,128)S(1)} %get-tuple-element.33.d_ref, f32[4,32,64,128]{3,2,1,0:T(8,128)S(1)} %get-tuple-element.26.refs_1_.fj_ref, f32[4,32,64,128]{3,2,1,0:T(8,128)S(1)} %get-tuple-element.27.refs_2_.fi_ref, f32[4,32,64,128]{3,2,1,0:T(8,128)S(1)} %get-tuple-element.28.refs_3_.fk_ref), custom_call_target="tpu_custom_call" | custom-call | flops 6291456 | bytes 5242880 | tf_op jit(solution)/shard_map/main/pallas_call | solution.py:246
  22.2 0.7 %main.9.refs_0_ = f32[4,32,64,128]{3,2,1,0:T(8,128)S(1)} custom-call(f32[4,32,64,128]{3,2,1,0:T(8,128)S(1)} %get-tuple-element.33.d_ref, f32[4,32,64,128]{3,2,1,0:T(8,128)S(1)} %get-tuple-element.26.refs_1_.fj_ref, f32[4,32,64,128]{3,2,1,0:T(8,128)S(1)} %get-tuple-element.27.refs_2_.fi_ref, ...), custom_call_target="tpu_custom_call", output_to_operand_aliasing={{}: (4, {})} | custom-call | flops 6291456 | bytes 5242880 | tf_op jit(solution)/shard_map/main/pallas_call | solution.py:246
  23.0 0.7 %main.10.refs_0_ = f32[4,32,64,128]{3,2,1,0:T(8,128)S(1)} custom-call(f32[4,32,64,128]{3,2,1,0:T(8,128)S(1)} %get-tuple-element.33.d_ref, f32[4,32,64,128]{3,2,1,0:T(8,128)S(1)} %get-tuple-element.26.refs_1_.fj_ref, f32[4,32,64,128]{3,2,1,0:T(8,128)S(1)} %get-tuple-element.27.refs_2_.fi_ref, ...), custom_call_target="tpu_custom_call", output_to_operand_aliasing={{}: (4, {})} | custom-call | flops 6291456 | bytes 5242880 | tf_op jit(solution)/shard_map/main/pallas_call | solution.py:246
  23.7 0.7 %main.11.refs_0_ = f32[4,32,64,128]{3,2,1,0:T(8,128)S(1)} custom-call(f32[4,32,64,128]{3,2,1,0:T(8,128)S(1)} %get-tuple-element.33.d_ref, f32[4,32,64,128]{3,2,1,0:T(8,128)S(1)} %get-tuple-element.26.refs_1_.fj_ref, f32[4,32,64,128]{3,2,1,0:T(8,128)S(1)} %get-tuple-element.27.refs_2_.fi_ref, ...), custom_call_target="tpu_custom_call", output_to_operand_aliasing={{}: (4, {})} | custom-call | flops 6291456 | bytes 5242880 | tf_op jit(solution)/shard_map/main/pallas_call | solution.py:246
  24.4 0.8 %collective-permute-done.7.refs_7_ = f32[4,32,128]{2,1,0:T(8,128)S(1)} collective-permute-done((f32[4,32,128]{2,1,0:T(8,128)S(1)}, f32[4,32,128]{2,1,0:T(8,128)S(1)}, u32[]{:S(2)}, u32[]{:S(2)}) %collective-permute-start.7) | collective-permute-done | bytes 65568 | tf_op jit(solution)/shard_map/ppermute | solution.py:26
  25.2 1.0 %patch.4 = (f32[4,32,64,128]{3,2,1,0:T(8,128)S(1)}, f32[32,64,128]{2,1,0:T(8,128)S(1)}, f32[4,64,128]{2,1,0:T(8,128)S(1)}, f32[4,64,128]{2,1,0:T(8,128)S(1)}, f32[4,32,128]{2,1,0:T(8,128)S(1)}) custom-call(f32[4,32,64,128]{3,2,1,0:T(8,128)S(1)} %main.11.refs_0_, ...), custom_call_target="tpu_custom_call", output_to_operand_aliasing={{0}: (0, {})} | custom-call | flops 1048576 | bytes 1048576 | tf_op jit(solution)/shard_map/patch/pallas_call | solution.py:204
  26.2 0.1 collective-permute-start.8
  26.3 2.8 %collective-permute-start.9 = (f32[4,64,128]{2,1,0:T(8,128)S(1)}, f32[4,64,128]{2,1,0:T(8,128)S(1)}, u32[]{:S(2)}, u32[]{:S(2)}) collective-permute-start(f32[4,64,128]{2,1,0:T(8,128)S(1)} %get-tuple-element.40), channel_id=1, source_target_pairs={{0,4},{8,12},{4,0},{12,8},{1,5},{9,13},{5,1},{13,9},{2,6},{10,14},... | collective-permute-start | bytes 393224 | tf_op jit(solution)/shard_map/ppermute | solution.py:26
  29.0 0.7 %collective-permute-start.10 = (f32[4,64,128]{2,1,0:T(8,128)S(1)}, f32[4,64,128]{2,1,0:T(8,128)S(1)}, u32[]{:S(2)}, u32[]{:S(2)}) collective-permute-start(f32[4,64,128]{2,1,0:T(8,128)S(1)} %get-tuple-element.41), channel_id=1, source_target_pairs={{4,8},{8,4},{5,9},{9,5},{6,10},{10,6},{7,11},{11,7},{20,24},{24,20... | collective-permute-start | bytes 393224 | tf_op jit(solution)/shard_map/ppermute | solution.py:26
  29.7 0.6 %collective-permute-start.11 = (f32[4,32,128]{2,1,0:T(8,128)S(1)}, f32[4,32,128]{2,1,0:T(8,128)S(1)}, u32[]{:S(2)}, u32[]{:S(2)}) collective-permute-start(f32[4,32,128]{2,1,0:T(8,128)S(1)} %get-tuple-element.42), channel_id=1, source_target_pairs={{0,2},{2,0},{1,3},{3,1},{4,6},{6,4},{5,7},{7,5},{8,10},{10,8},{9,1... | collective-permute-start | bytes 196616 | tf_op jit(solution)/shard_map/ppermute | solution.py:26
  30.3 0.7 %main.12.refs_0_ = f32[4,32,64,128]{3,2,1,0:T(8,128)S(1)} custom-call(f32[4,32,64,128]{3,2,1,0:T(8,128)S(1)} %get-tuple-element.38.d_ref, f32[4,32,64,128]{3,2,1,0:T(8,128)S(1)} %get-tuple-element.26.refs_1_.fj_ref, f32[4,32,64,128]{3,2,1,0:T(8,128)S(1)} %get-tuple-element.27.refs_2_.fi_ref, f32[4,32,64,128]{3,2,1,0:T(8,128)S(1)} %get-tuple-element.28.refs_3_.fk_ref), custom_call_target="tpu_custom_call" | custom-call | flops 6291456 | bytes 5242880 | tf_op jit(solution)/shard_map/main/pallas_call | solution.py:246
  31.0 0.7 %main.13.refs_0_ = f32[4,32,64,128]{3,2,1,0:T(8,128)S(1)} custom-call(f32[4,32,64,128]{3,2,1,0:T(8,128)S(1)} %get-tuple-element.38.d_ref, f32[4,32,64,128]{3,2,1,0:T(8,128)S(1)} %get-tuple-element.26.refs_1_.fj_ref, f32[4,32,64,128]{3,2,1,0:T(8,128)S(1)} %get-tuple-element.27.refs_2_.fi_ref, ...), custom_call_target="tpu_custom_call", output_to_operand_aliasing={{}: (4, {})} | custom-call | flops 6291456 | bytes 5242880 | tf_op jit(solution)/shard_map/main/pallas_call | solution.py:246
  31.8 0.7 %main.14.refs_0_ = f32[4,32,64,128]{3,2,1,0:T(8,128)S(1)} custom-call(f32[4,32,64,128]{3,2,1,0:T(8,128)S(1)} %get-tuple-element.38.d_ref, f32[4,32,64,128]{3,2,1,0:T(8,128)S(1)} %get-tuple-element.26.refs_1_.fj_ref, f32[4,32,64,128]{3,2,1,0:T(8,128)S(1)} %get-tuple-element.27.refs_2_.fi_ref, ...), custom_call_target="tpu_custom_call", output_to_operand_aliasing={{}: (4, {})} | custom-call | flops 6291456 | bytes 5242880 | tf_op jit(solution)/shard_map/main/pallas_call | solution.py:246
  32.5 0.7 %main.15.refs_0_ = f32[4,32,64,128]{3,2,1,0:T(8,128)S(1)} custom-call(f32[4,32,64,128]{3,2,1,0:T(8,128)S(1)} %get-tuple-element.38.d_ref, f32[4,32,64,128]{3,2,1,0:T(8,128)S(1)} %get-tuple-element.26.refs_1_.fj_ref, f32[4,32,64,128]{3,2,1,0:T(8,128)S(1)} %get-tuple-element.27.refs_2_.fi_ref, ...), custom_call_target="tpu_custom_call", output_to_operand_aliasing={{}: (4, {})} | custom-call | flops 6291456 | bytes 5242880 | tf_op jit(solution)/shard_map/main/pallas_call | solution.py:246
  33.3 0.8 %collective-permute-done.11.refs_7_ = f32[4,32,128]{2,1,0:T(8,128)S(1)} collective-permute-done((f32[4,32,128]{2,1,0:T(8,128)S(1)}, f32[4,32,128]{2,1,0:T(8,128)S(1)}, u32[]{:S(2)}, u32[]{:S(2)}) %collective-permute-start.11) | collective-permute-done | bytes 65568 | tf_op jit(solution)/shard_map/ppermute | solution.py:26
  34.0 0.7 %patch.5 = f32[4,32,64,128]{3,2,1,0:T(8,128)S(1)} custom-call(f32[4,32,64,128]{3,2,1,0:T(8,128)S(1)} %main.15.refs_0_, f32[4,32,64,128]{3,2,1,0:T(8,128)S(1)} %get-tuple-element.26.refs_1_.fj_ref, f32[4,32,64,128]{3,2,1,0:T(8,128)S(1)} %get-tuple-element.27.refs_2_.fi_ref, ...), custom_call_target="tpu_custom_call", output_to_operand_aliasing={{}: (0, {})} | custom-call | flops 1048576 | bytes 1048576 | tf_op jit(solution)/shard_map/patch/pallas_call | solution.py:204
  34.8 2.0 %copy.23 = f32[4,32,64,128]{3,2,1,0:T(8,128)} copy(f32[4,32,64,128]{3,2,1,0:T(8,128)S(1)} %patch.5) | data formatting | bytes 8388608
  (12 shorter events, 0.0 us)
Async XLA Ops:
  0.0 2.2 %copy-start = (f32[4,32,64,128]{3,2,1,0:T(8,128)S(1)}, f32[4,32,64,128]{3,2,1,0:T(8,128)}, u32[]{:S(2)}) copy-start(f32[4,32,64,128]{3,2,1,0:T(8,128)} %x_ref.1) | copy-start | bytes 12582916
  2.2 6.0 %copy-start.1 = (f32[4,32,64,128]{3,2,1,0:T(8,128)S(1)}, f32[4,32,64,128]{3,2,1,0:T(8,128)}, u32[]{:S(2)}) copy-start(f32[4,32,64,128]{3,2,1,0:T(8,128)} %fj_hbm.1) | copy-start | bytes 12582916
  2.8 11.9 %collective-permute-start = (f32[32,64,128]{2,1,0:T(8,128)S(1)}, f32[32,64,128]{2,1,0:T(8,128)S(1)}, u32[]{:S(2)}, u32[]{:S(2)}) collective-permute-start(f32[32,64,128]{2,1,0:T(8,128)S(1)} %get-tuple-element.29), channel_id=1, source_target_pairs={{0,16},{16,0},{1,17},{17,1},{2,18},{18,2},{3,19},{19,3},{4,20},{20... | collective-permute-start | bytes 3145736 | tf_op jit(solution)/shard_map/ppermute | solution.py:26
  3.3 11.3 %collective-permute-start.1 = (f32[4,64,128]{2,1,0:T(8,128)S(1)}, f32[4,64,128]{2,1,0:T(8,128)S(1)}, u32[]{:S(2)}, u32[]{:S(2)}) collective-permute-start(f32[4,64,128]{2,1,0:T(8,128)S(1)} %get-tuple-element.30), channel_id=1, source_target_pairs={{0,4},{8,12},{4,0},{12,8},{1,5},{9,13},{5,1},{13,9},{2,6},{10,14},... | collective-permute-start | bytes 393224 | tf_op jit(solution)/shard_map/ppermute | solution.py:26
  6.0 8.7 %collective-permute-start.2 = (f32[4,64,128]{2,1,0:T(8,128)S(1)}, f32[4,64,128]{2,1,0:T(8,128)S(1)}, u32[]{:S(2)}, u32[]{:S(2)}) collective-permute-start(f32[4,64,128]{2,1,0:T(8,128)S(1)} %get-tuple-element.31), channel_id=1, source_target_pairs={{4,8},{8,4},{5,9},{9,5},{6,10},{10,6},{7,11},{11,7},{20,24},{24,20... | collective-permute-start | bytes 393224 | tf_op jit(solution)/shard_map/ppermute | solution.py:26
  6.6 8.0 %collective-permute-start.3 = (f32[4,32,128]{2,1,0:T(8,128)S(1)}, f32[4,32,128]{2,1,0:T(8,128)S(1)}, u32[]{:S(2)}, u32[]{:S(2)}) collective-permute-start(f32[4,32,128]{2,1,0:T(8,128)S(1)} %get-tuple-element.32), channel_id=1, source_target_pairs={{0,2},{2,0},{1,3},{3,1},{4,6},{6,4},{5,7},{7,5},{8,10},{10,8},{9,1... | collective-permute-start | bytes 196616 | tf_op jit(solution)/shard_map/ppermute | solution.py:26
  8.2 2.2 %copy-start.2 = (f32[4,32,64,128]{3,2,1,0:T(8,128)S(1)}, f32[4,32,64,128]{3,2,1,0:T(8,128)}, u32[]{:S(2)}) copy-start(f32[4,32,64,128]{3,2,1,0:T(8,128)} %fi_hbm.1) | copy-start | bytes 12582916
  15.7 9.5 %collective-permute-start.4 = (f32[32,64,128]{2,1,0:T(8,128)S(1)}, f32[32,64,128]{2,1,0:T(8,128)S(1)}, u32[]{:S(2)}, u32[]{:S(2)}) collective-permute-start(f32[32,64,128]{2,1,0:T(8,128)S(1)} %get-tuple-element.34), channel_id=1, source_target_pairs={{0,16},{16,0},{1,17},{17,1},{2,18},{18,2},{3,19},{19,3},{4,20},{20... | collective-permute-start | bytes 3145736 | tf_op jit(solution)/shard_map/ppermute | solution.py:26
  15.8 9.5 %collective-permute-start.5 = (f32[4,64,128]{2,1,0:T(8,128)S(1)}, f32[4,64,128]{2,1,0:T(8,128)S(1)}, u32[]{:S(2)}, u32[]{:S(2)}) collective-permute-start(f32[4,64,128]{2,1,0:T(8,128)S(1)} %get-tuple-element.35), channel_id=1, source_target_pairs={{0,4},{8,12},{4,0},{12,8},{1,5},{9,13},{5,1},{13,9},{2,6},{10,14},... | collective-permute-start | bytes 393224 | tf_op jit(solution)/shard_map/ppermute | solution.py:26
  20.2 5.0 %collective-permute-start.6 = (f32[4,64,128]{2,1,0:T(8,128)S(1)}, f32[4,64,128]{2,1,0:T(8,128)S(1)}, u32[]{:S(2)}, u32[]{:S(2)}) collective-permute-start(f32[4,64,128]{2,1,0:T(8,128)S(1)} %get-tuple-element.36), channel_id=1, source_target_pairs={{4,8},{8,4},{5,9},{9,5},{6,10},{10,6},{7,11},{11,7},{20,24},{24,20... | collective-permute-start | bytes 393224 | tf_op jit(solution)/shard_map/ppermute | solution.py:26
  20.9 4.3 %collective-permute-start.7 = (f32[4,32,128]{2,1,0:T(8,128)S(1)}, f32[4,32,128]{2,1,0:T(8,128)S(1)}, u32[]{:S(2)}, u32[]{:S(2)}) collective-permute-start(f32[4,32,128]{2,1,0:T(8,128)S(1)} %get-tuple-element.37), channel_id=1, source_target_pairs={{0,2},{2,0},{1,3},{3,1},{4,6},{6,4},{5,7},{7,5},{8,10},{10,8},{9,1... | collective-permute-start | bytes 196616 | tf_op jit(solution)/shard_map/ppermute | solution.py:26
  26.2 7.8 %collective-permute-start.8 = (f32[32,64,128]{2,1,0:T(8,128)S(1)}, f32[32,64,128]{2,1,0:T(8,128)S(1)}, u32[]{:S(2)}, u32[]{:S(2)}) collective-permute-start(f32[32,64,128]{2,1,0:T(8,128)S(1)} %get-tuple-element.39), channel_id=1, source_target_pairs={{0,16},{16,0},{1,17},{17,1},{2,18},{18,2},{3,19},{19,3},{4,20},{20... | collective-permute-start | bytes 3145736 | tf_op jit(solution)/shard_map/ppermute | solution.py:26
  26.3 7.8 %collective-permute-start.9 = (f32[4,64,128]{2,1,0:T(8,128)S(1)}, f32[4,64,128]{2,1,0:T(8,128)S(1)}, u32[]{:S(2)}, u32[]{:S(2)}) collective-permute-start(f32[4,64,128]{2,1,0:T(8,128)S(1)} %get-tuple-element.40), channel_id=1, source_target_pairs={{0,4},{8,12},{4,0},{12,8},{1,5},{9,13},{5,1},{13,9},{2,6},{10,14},... | collective-permute-start | bytes 393224 | tf_op jit(solution)/shard_map/ppermute | solution.py:26
  29.0 5.0 %collective-permute-start.10 = (f32[4,64,128]{2,1,0:T(8,128)S(1)}, f32[4,64,128]{2,1,0:T(8,128)S(1)}, u32[]{:S(2)}, u32[]{:S(2)}) collective-permute-start(f32[4,64,128]{2,1,0:T(8,128)S(1)} %get-tuple-element.41), channel_id=1, source_target_pairs={{4,8},{8,4},{5,9},{9,5},{6,10},{10,6},{7,11},{11,7},{20,24},{24,20... | collective-permute-start | bytes 393224 | tf_op jit(solution)/shard_map/ppermute | solution.py:26
  29.7 4.3 %collective-permute-start.11 = (f32[4,32,128]{2,1,0:T(8,128)S(1)}, f32[4,32,128]{2,1,0:T(8,128)S(1)}, u32[]{:S(2)}, u32[]{:S(2)}) collective-permute-start(f32[4,32,128]{2,1,0:T(8,128)S(1)} %get-tuple-element.42), channel_id=1, source_target_pairs={{0,2},{2,0},{1,3},{3,1},{4,6},{6,4},{5,7},{7,5},{8,10},{10,8},{9,1... | collective-permute-start | bytes 196616 | tf_op jit(solution)/shard_map/ppermute | solution.py:26

commit v4 on v2

--- a/solution.py
+++ b/solution.py
@@ -151,25 +151,46 @@
     nj, ni, nk, _ = d_ref.shape
     tile = 8
     row = lax.broadcasted_iota(jnp.int32, (tile, d_ref.shape[3]), 0)
+    rows_k = []
     for (start, sign), halo in zip(sides(2, counts[2], nk, tile), halos[2]):
         start = pl.multiple_of(start, tile)
         mask = jnp.where(row == jnp.where(sign > 0, 0, tile - 1), 1.0, 0.0)
-        for j in range(nj):
+        rows_k.append((start, sign, mask, halo))
+
+    def plane(j):
+        for start, sign, mask, halo in rows_k:
 
             @pl.loop(0, ni, unroll=8)
-            def _(i, j=j, start=start, sign=sign, mask=mask, halo=halo):
+            def _(i, start=start, sign=sign, mask=mask, halo=halo):
                 weight = (RATE + sign * fk_ref[j, i, pl.ds(start, tile)]) * mask
                 o_ref[j, i, pl.ds(start, tile)] = d_ref[j, i, pl.ds(start, tile)] + weight * halo[j, pl.ds(i, 1)]
 
-    for (at, sign), halo in zip(sides(1, counts[1], ni), halos[1]):
-        for j in range(nj):
+        for (at, sign), halo in zip(sides(1, counts[1], ni), halos[1]):
             o_ref[j, at] = o_ref[j, at] + (RATE + sign * fi_ref[j, at]) * halo[j]
-    for (at, sign), halo in zip(sides(0, counts[0], nj), halos[0]):
+    outer = sides(0, counts[0], nj)
+    order = [lax.rem(outer[0][0] + n, nj) for n in range(1, nj + 1)] if len(outer) == 1 else list(range(nj))
+    early = nj - 1 if len(outer) == 1 else 0 if outer else nj
+    copies = []
+
+    def send(n):
+        if not emit:
+            copies.append(pltpu.make_async_copy(o_ref.at[order[n]], refs[5 + size].at[order[n]], refs[-1].at[n]))
+            copies[-1].start()
+
+    for n in range(nj):
+        plane(order[n])
+        if n < early:
+            send(n)
+    for (at, sign), halo in zip(outer, halos[0]):
 
         @pl.loop(0, ni, unroll=2)
         def _(i, at=at, sign=sign, halo=halo):
             o_ref[at, i] = o_ref[at, i] + (RATE + sign * fj_ref[at, i]) * halo[i]
 
+    for n in range(early, nj):
+        send(n)
+    for copy in copies:
+        copy.wait()
     if emit:
         faces = grouped(refs[5 + size :], counts)
         copy_face_j(counts, o_ref, faces)
@@ -195,13 +216,14 @@
 
     def patch(x, halos, emit):
         flat = [h for hs in halos for h in hs]
-        outs = [whole] + (faces_out if emit else [])
+        outs = [whole] + (faces_out if emit else [pltpu.HBM(shape, dtype)])
         got = pl.pallas_call(
             functools.partial(patch_kernel, counts, emit),
             out_shape=outs,
             in_specs=[VM] * (4 + len(flat)),
-            out_specs=[VM] * len(outs),
+            out_specs=[VM] * len(outs) if emit else [VM, HBM],
             input_output_aliases={0: 0},
+            scratch_shapes=[] if emit else [pltpu.SemaphoreType.DMA((shape[0],))],
             name="patch",
             compiler_params=params,
             cost_estimate=cost(1, 1),
@@ -231,7 +253,7 @@
                 out_specs=[VM] * 4,
                 scratch_shapes=[pltpu.SemaphoreType.DMA((3, PIECES if shape[1] % PIECES == 0 else 1))],
                 name="first",
-                compiler_params=params,
+                compiler_params=pltpu.CompilerParams(vmem_limit_bytes=28 * 2**20),
                 cost_estimate=cost(24, 20),
             )(density, *flows)
         else:
@@ -245,7 +267,7 @@
                 cost_estimate=cost(24, 20),
             )(density, *flows)
         density, faces = patch(density, halos, step < STEPS - 1)
-    return density
+    return faces[0]
 
 
 def solution(mesh):

time: 37 us -> 34.6 us (0.935)
  local copies, waits for them, and re-layouts: 6.39 us -> 2.19 us
  Pallas kernels: 13.3 us -> 15.2 us
    unnamed x7 -> x4, local copies, waits for them, and re-layouts: 6.39 us -> 2.19 us
    pallas_call x3, Pallas kernels: 2.63 us -> 4.34 us  [patch(): pl.pallas_call(functools.partial(patch_kernel, counts, emit), out_shape=o...]
  transfers between devices with their start and end apart: 12 -> 12, of which waited for: 2 -> 2; matrix products, arithmetic and copies ran while one was open for 0% -> 0% of each run, Pallas kernels for 28% -> 30%
where the time goes in v4:
time: 34.6 us; the launch traced here: 34.4 us
  starting transfers between devices  15.3 us (44%)
  Pallas kernels  15.2 us (44%)
  local copies, waits for them, and re-layouts  2.19 us (6%)
  waiting for transfers between devices  1.62 us (5%)
    ppermute x12, starting transfers between devices, exchange(): lax.ppermute(face, axis, up + [(j, i) for i, j in up])  15.3 us
    pallas_call x2, Pallas kernels, per_device(): pl.pallas_call(main_kernel, out_shape=whole, in_specs=[VM] * 4, out_specs...  5.85 us
    pallas_call x1, Pallas kernels, per_device(): pl.pallas_call(first_kernel, out_shape=[whole] * 4, in_specs=[VM] + [HBM]...  4.39 us
    pallas_call x3, Pallas kernels, patch(): pl.pallas_call(functools.partial(patch_kernel, counts, emit), out_shape=o...  4.34 us
    unnamed x4, local copies, waits for them, and re-layouts  2.19 us
    ppermute x12, waiting for transfers between devices, exchange(): lax.ppermute(face, axis, up + [(j, i) for i, j in up])  1.62 us
  transfers between devices with their start and end apart: 12, of which 2 were waited for; matrix products, arithmetic and copies ran while one was open for 0% of the time, Pallas kernels for 30%

profile of v4, /device:TPU:0, one launch (start us, length us, event | category | flops | bytes accessed | tf_op | source)
XLA Modules:
  0.0 34.4 jit_solution(14517570024614596572)
XLA Ops:
  0.0 2.2 %copy-done = f32[4,32,64,128]{3,2,1,0:T(8,128)S(1)} copy-done((f32[4,32,64,128]{3,2,1,0:T(8,128)S(1)}, f32[4,32,64,128]{3,2,1,0:T(8,128)}, u32[]{:S(2)}) %copy-start) | copy-done | bytes 4194328
  2.2 0.6 %load.1 = (f32[4,32,64,128]{3,2,1,0:T(8,128)S(1)}, f32[32,64,128]{2,1,0:T(8,128)S(1)}, f32[4,64,128]{2,1,0:T(8,128)S(1)}, f32[4,64,128]{2,1,0:T(8,128)S(1)}, f32[4,32,128]{2,1,0:T(8,128)S(1)}) custom-call(f32[4,32,64,128]{3,2,1,0:T(8,128)S(1)} %copy-done), custom_call_target="tpu_custom_call" | custom-call | flops 1048576 | bytes 4194304 | tf_op jit(solution)/shard_map/load/pallas_call | solution.py:233
  2.8 0.6 %collective-permute-start = (f32[32,64,128]{2,1,0:T(8,128)S(1)}, f32[32,64,128]{2,1,0:T(8,128)S(1)}, u32[]{:S(2)}, u32[]{:S(2)}) collective-permute-start(f32[32,64,128]{2,1,0:T(8,128)S(1)} %get-tuple-element.30), channel_id=1, source_target_pairs={{0,16},{16,0},{1,17},{17,1},{2,18},{18,2},{3,19},{19,3},{4,20},{20... | collective-permute-start | bytes 3145736 | tf_op jit(solution)/shard_map/ppermute | solution.py:22
  3.3 2.6 %collective-permute-start.1 = (f32[4,64,128]{2,1,0:T(8,128)S(1)}, f32[4,64,128]{2,1,0:T(8,128)S(1)}, u32[]{:S(2)}, u32[]{:S(2)}) collective-permute-start(f32[4,64,128]{2,1,0:T(8,128)S(1)} %get-tuple-element.31), channel_id=1, source_target_pairs={{0,4},{8,12},{4,0},{12,8},{1,5},{9,13},{5,1},{13,9},{2,6},{10,14},... | collective-permute-start | bytes 393224 | tf_op jit(solution)/shard_map/ppermute | solution.py:22
  6.0 0.7 %collective-permute-start.2 = (f32[4,64,128]{2,1,0:T(8,128)S(1)}, f32[4,64,128]{2,1,0:T(8,128)S(1)}, u32[]{:S(2)}, u32[]{:S(2)}) collective-permute-start(f32[4,64,128]{2,1,0:T(8,128)S(1)} %get-tuple-element.32), channel_id=1, source_target_pairs={{4,8},{8,4},{5,9},{9,5},{6,10},{10,6},{7,11},{11,7},{20,24},{24,20... | collective-permute-start | bytes 393224 | tf_op jit(solution)/shard_map/ppermute | solution.py:22
  6.6 1.6 %collective-permute-start.3 = (f32[4,32,128]{2,1,0:T(8,128)S(1)}, f32[4,32,128]{2,1,0:T(8,128)S(1)}, u32[]{:S(2)}, u32[]{:S(2)}) collective-permute-start(f32[4,32,128]{2,1,0:T(8,128)S(1)} %get-tuple-element.33), channel_id=1, source_target_pairs={{0,2},{2,0},{1,3},{3,1},{4,6},{6,4},{5,7},{7,5},{8,10},{10,8},{9,1... | collective-permute-start | bytes 196616 | tf_op jit(solution)/shard_map/ppermute | solution.py:22
  8.2 4.4 %first.1 = (f32[4,32,64,128]{3,2,1,0:T(8,128)S(1)}, f32[4,32,64,128]{3,2,1,0:T(8,128)S(1)}, f32[4,32,64,128]{3,2,1,0:T(8,128)S(1)}, f32[4,32,64,128]{3,2,1,0:T(8,128)S(1)}) custom-call(f32[4,32,64,128]{3,2,1,0:T(8,128)S(1)} %get-tuple-element.25.d_ref, f32[4,32,64,128]{3,2,1,0:T(8,128)S(1)} %copy-done.1, f32[4,32,64,128]{3,2,1,0:T(8,128)} %fi_hbm.1, ...), custom_call_target="tpu_custom_call" | custom-call | flops 25165824 | bytes 20971520 | tf_op jit(solution)/shard_map/first/pallas_call | solution.py:249
  12.6 0.0 collective-permute-done.3.refs_7_
  12.6 0.0 collective-permute-done.1.refs_5_
  12.6 0.0 collective-permute-done.2.refs_6_
  12.6 0.0 collective-permute-done.refs_4_
  12.6 1.1 %patch.3 = (f32[4,32,64,128]{3,2,1,0:T(8,128)S(1)}, f32[32,64,128]{2,1,0:T(8,128)S(1)}, f32[4,64,128]{2,1,0:T(8,128)S(1)}, f32[4,64,128]{2,1,0:T(8,128)S(1)}, f32[4,32,128]{2,1,0:T(8,128)S(1)}) custom-call(f32[4,32,64,128]{3,2,1,0:T(8,128)S(1)} %get-tuple-element.26.refs_0_, ...), custom_call_target="tpu_custom_call", output_to_operand_aliasing={{0}: (0, {})} | custom-call | flops 1048576 | bytes 1048576 | tf_op jit(solution)/shard_map/patch/pallas_call | solution.py:220
  13.7 0.1 collective-permute-start.4
  13.8 4.5 %collective-permute-start.5 = (f32[4,64,128]{2,1,0:T(8,128)S(1)}, f32[4,64,128]{2,1,0:T(8,128)S(1)}, u32[]{:S(2)}, u32[]{:S(2)}) collective-permute-start(f32[4,64,128]{2,1,0:T(8,128)S(1)} %get-tuple-element.36), channel_id=1, source_target_pairs={{0,4},{8,12},{4,0},{12,8},{1,5},{9,13},{5,1},{13,9},{2,6},{10,14},... | collective-permute-start | bytes 393224 | tf_op jit(solution)/shard_map/ppermute | solution.py:22
  18.3 0.7 %collective-permute-start.6 = (f32[4,64,128]{2,1,0:T(8,128)S(1)}, f32[4,64,128]{2,1,0:T(8,128)S(1)}, u32[]{:S(2)}, u32[]{:S(2)}) collective-permute-start(f32[4,64,128]{2,1,0:T(8,128)S(1)} %get-tuple-element.37), channel_id=1, source_target_pairs={{4,8},{8,4},{5,9},{9,5},{6,10},{10,6},{7,11},{11,7},{20,24},{24,20... | collective-permute-start | bytes 393224 | tf_op jit(solution)/shard_map/ppermute | solution.py:22
  18.9 0.6 %collective-permute-start.7 = (f32[4,32,128]{2,1,0:T(8,128)S(1)}, f32[4,32,128]{2,1,0:T(8,128)S(1)}, u32[]{:S(2)}, u32[]{:S(2)}) collective-permute-start(f32[4,32,128]{2,1,0:T(8,128)S(1)} %get-tuple-element.38), channel_id=1, source_target_pairs={{0,2},{2,0},{1,3},{3,1},{4,6},{6,4},{5,7},{7,5},{8,10},{10,8},{9,1... | collective-permute-start | bytes 196616 | tf_op jit(solution)/shard_map/ppermute | solution.py:22
  19.5 2.9 %main.2.refs_0_ = f32[4,32,64,128]{3,2,1,0:T(8,128)S(1)} custom-call(f32[4,32,64,128]{3,2,1,0:T(8,128)S(1)} %get-tuple-element.34.d_ref, f32[4,32,64,128]{3,2,1,0:T(8,128)S(1)} %get-tuple-element.27.refs_1_.fj_ref, f32[4,32,64,128]{3,2,1,0:T(8,128)S(1)} %get-tuple-element.28.refs_2_.fi_ref, f32[4,32,64,128]{3,2,1,0:T(8,128)S(1)} %get-tuple-element.29.refs_3_.fk_ref), custom_call_target="tpu_custom_call" | custom-call | flops 25165824 | bytes 20971520 | tf_op jit(solution)/shard_map/main/pallas_call | solution.py:260
  22.5 0.8 %collective-permute-done.7.refs_7_ = f32[4,32,128]{2,1,0:T(8,128)S(1)} collective-permute-done((f32[4,32,128]{2,1,0:T(8,128)S(1)}, f32[4,32,128]{2,1,0:T(8,128)S(1)}, u32[]{:S(2)}, u32[]{:S(2)}) %collective-permute-start.7) | collective-permute-done | bytes 65568 | tf_op jit(solution)/shard_map/ppermute | solution.py:22
  23.3 0.0 collective-permute-done.5.refs_5_
  23.3 0.0 collective-permute-done.6.refs_6_
  23.3 0.0 collective-permute-done.4.refs_4_
  23.3 1.1 %patch.4 = (f32[4,32,64,128]{3,2,1,0:T(8,128)S(1)}, f32[32,64,128]{2,1,0:T(8,128)S(1)}, f32[4,64,128]{2,1,0:T(8,128)S(1)}, f32[4,64,128]{2,1,0:T(8,128)S(1)}, f32[4,32,128]{2,1,0:T(8,128)S(1)}) custom-call(f32[4,32,64,128]{3,2,1,0:T(8,128)S(1)} %main.2.refs_0_, ...), custom_call_target="tpu_custom_call", output_to_operand_aliasing={{0}: (0, {})} | custom-call | flops 1048576 | bytes 1048576 | tf_op jit(solution)/shard_map/patch/pallas_call | solution.py:220
  24.4 0.1 collective-permute-start.8
  24.4 2.7 %collective-permute-start.9 = (f32[4,64,128]{2,1,0:T(8,128)S(1)}, f32[4,64,128]{2,1,0:T(8,128)S(1)}, u32[]{:S(2)}, u32[]{:S(2)}) collective-permute-start(f32[4,64,128]{2,1,0:T(8,128)S(1)} %get-tuple-element.41), channel_id=1, source_target_pairs={{0,4},{8,12},{4,0},{12,8},{1,5},{9,13},{5,1},{13,9},{2,6},{10,14},... | collective-permute-start | bytes 393224 | tf_op jit(solution)/shard_map/ppermute | solution.py:22
  27.2 0.7 %collective-permute-start.10 = (f32[4,64,128]{2,1,0:T(8,128)S(1)}, f32[4,64,128]{2,1,0:T(8,128)S(1)}, u32[]{:S(2)}, u32[]{:S(2)}) collective-permute-start(f32[4,64,128]{2,1,0:T(8,128)S(1)} %get-tuple-element.42), channel_id=1, source_target_pairs={{4,8},{8,4},{5,9},{9,5},{6,10},{10,6},{7,11},{11,7},{20,24},{24,20... | collective-permute-start | bytes 393224 | tf_op jit(solution)/shard_map/ppermute | solution.py:22
  27.8 0.6 %collective-permute-start.11 = (f32[4,32,128]{2,1,0:T(8,128)S(1)}, f32[4,32,128]{2,1,0:T(8,128)S(1)}, u32[]{:S(2)}, u32[]{:S(2)}) collective-permute-start(f32[4,32,128]{2,1,0:T(8,128)S(1)} %get-tuple-element.43), channel_id=1, source_target_pairs={{0,2},{2,0},{1,3},{3,1},{4,6},{6,4},{5,7},{7,5},{8,10},{10,8},{9,1... | collective-permute-start | bytes 196616 | tf_op jit(solution)/shard_map/ppermute | solution.py:22
  28.4 2.9 %main.3.refs_0_ = f32[4,32,64,128]{3,2,1,0:T(8,128)S(1)} custom-call(f32[4,32,64,128]{3,2,1,0:T(8,128)S(1)} %get-tuple-element.39.d_ref, f32[4,32,64,128]{3,2,1,0:T(8,128)S(1)} %get-tuple-element.27.refs_1_.fj_ref, f32[4,32,64,128]{3,2,1,0:T(8,128)S(1)} %get-tuple-element.28.refs_2_.fi_ref, f32[4,32,64,128]{3,2,1,0:T(8,128)S(1)} %get-tuple-element.29.refs_3_.fk_ref), custom_call_target="tpu_custom_call" | custom-call | flops 25165824 | bytes 20971520 | tf_op jit(solution)/shard_map/main/pallas_call | solution.py:260
  31.4 0.8 %collective-permute-done.11.refs_7_ = f32[4,32,128]{2,1,0:T(8,128)S(1)} collective-permute-done((f32[4,32,128]{2,1,0:T(8,128)S(1)}, f32[4,32,128]{2,1,0:T(8,128)S(1)}, u32[]{:S(2)}, u32[]{:S(2)}) %collective-permute-start.11) | collective-permute-done | bytes 65568 | tf_op jit(solution)/shard_map/ppermute | solution.py:22
  32.2 0.0 collective-permute-done.9.refs_5_
  32.2 0.0 collective-permute-done.10.refs_6_
  32.2 0.0 collective-permute-done.8.refs_4_
  32.2 2.2 %patch.5 = (f32[4,32,64,128]{3,2,1,0:T(8,128)S(1)}, f32[4,32,64,128]{3,2,1,0:T(8,128)}) custom-call(f32[4,32,64,128]{3,2,1,0:T(8,128)S(1)} %main.3.refs_0_, f32[4,32,64,128]{3,2,1,0:T(8,128)S(1)} %get-tuple-element.27.refs_1_.fj_ref, f32[4,32,64,128]{3,2,1,0:T(8,128)S(1)} %get-tuple-element.28.refs_2_.fi_ref, ...), custom_call_target="tpu_custom_call", output_to_operand_aliasing={{0}: (0, {})} | custom-call | flops 1048576 | bytes 1048576 | tf_op jit(solution)/shard_map/patch/pallas_call | solution.py:220
  (3 shorter events, 0.0 us)
Async XLA Ops:
  0.0 2.2 %copy-start = (f32[4,32,64,128]{3,2,1,0:T(8,128)S(1)}, f32[4,32,64,128]{3,2,1,0:T(8,128)}, u32[]{:S(2)}) copy-start(f32[4,32,64,128]{3,2,1,0:T(8,128)} %x_ref.1) | copy-start | bytes 12582916
  2.2 6.0 %copy-start.1 = (f32[4,32,64,128]{3,2,1,0:T(8,128)S(1)}, f32[4,32,64,128]{3,2,1,0:T(8,128)}, u32[]{:S(2)}) copy-start(f32[4,32,64,128]{3,2,1,0:T(8,128)} %fj_hbm.1) | copy-start | bytes 12582916
  2.8 9.9 %collective-permute-start = (f32[32,64,128]{2,1,0:T(8,128)S(1)}, f32[32,64,128]{2,1,0:T(8,128)S(1)}, u32[]{:S(2)}, u32[]{:S(2)}) collective-permute-start(f32[32,64,128]{2,1,0:T(8,128)S(1)} %get-tuple-element.30), channel_id=1, source_target_pairs={{0,16},{16,0},{1,17},{17,1},{2,18},{18,2},{3,19},{19,3},{4,20},{20... | collective-permute-start | bytes 3145736 | tf_op jit(solution)/shard_map/ppermute | solution.py:22
  3.3 9.3 %collective-permute-start.1 = (f32[4,64,128]{2,1,0:T(8,128)S(1)}, f32[4,64,128]{2,1,0:T(8,128)S(1)}, u32[]{:S(2)}, u32[]{:S(2)}) collective-permute-start(f32[4,64,128]{2,1,0:T(8,128)S(1)} %get-tuple-element.31), channel_id=1, source_target_pairs={{0,4},{8,12},{4,0},{12,8},{1,5},{9,13},{5,1},{13,9},{2,6},{10,14},... | collective-permute-start | bytes 393224 | tf_op jit(solution)/shard_map/ppermute | solution.py:22
  6.0 6.6 %collective-permute-start.2 = (f32[4,64,128]{2,1,0:T(8,128)S(1)}, f32[4,64,128]{2,1,0:T(8,128)S(1)}, u32[]{:S(2)}, u32[]{:S(2)}) collective-permute-start(f32[4,64,128]{2,1,0:T(8,128)S(1)} %get-tuple-element.32), channel_id=1, source_target_pairs={{4,8},{8,4},{5,9},{9,5},{6,10},{10,6},{7,11},{11,7},{20,24},{24,20... | collective-permute-start | bytes 393224 | tf_op jit(solution)/shard_map/ppermute | solution.py:22
  6.6 6.0 %collective-permute-start.3 = (f32[4,32,128]{2,1,0:T(8,128)S(1)}, f32[4,32,128]{2,1,0:T(8,128)S(1)}, u32[]{:S(2)}, u32[]{:S(2)}) collective-permute-start(f32[4,32,128]{2,1,0:T(8,128)S(1)} %get-tuple-element.33), channel_id=1, source_target_pairs={{0,2},{2,0},{1,3},{3,1},{4,6},{6,4},{5,7},{7,5},{8,10},{10,8},{9,1... | collective-permute-start | bytes 196616 | tf_op jit(solution)/shard_map/ppermute | solution.py:22
  13.7 9.5 %collective-permute-start.4 = (f32[32,64,128]{2,1,0:T(8,128)S(1)}, f32[32,64,128]{2,1,0:T(8,128)S(1)}, u32[]{:S(2)}, u32[]{:S(2)}) collective-permute-start(f32[32,64,128]{2,1,0:T(8,128)S(1)} %get-tuple-element.35), channel_id=1, source_target_pairs={{0,16},{16,0},{1,17},{17,1},{2,18},{18,2},{3,19},{19,3},{4,20},{20... | collective-permute-start | bytes 3145736 | tf_op jit(solution)/shard_map/ppermute | solution.py:22
  13.8 9.5 %collective-permute-start.5 = (f32[4,64,128]{2,1,0:T(8,128)S(1)}, f32[4,64,128]{2,1,0:T(8,128)S(1)}, u32[]{:S(2)}, u32[]{:S(2)}) collective-permute-start(f32[4,64,128]{2,1,0:T(8,128)S(1)} %get-tuple-element.36), channel_id=1, source_target_pairs={{0,4},{8,12},{4,0},{12,8},{1,5},{9,13},{5,1},{13,9},{2,6},{10,14},... | collective-permute-start | bytes 393224 | tf_op jit(solution)/shard_map/ppermute | solution.py:22
  18.3 5.0 %collective-permute-start.6 = (f32[4,64,128]{2,1,0:T(8,128)S(1)}, f32[4,64,128]{2,1,0:T(8,128)S(1)}, u32[]{:S(2)}, u32[]{:S(2)}) collective-permute-start(f32[4,64,128]{2,1,0:T(8,128)S(1)} %get-tuple-element.37), channel_id=1, source_target_pairs={{4,8},{8,4},{5,9},{9,5},{6,10},{10,6},{7,11},{11,7},{20,24},{24,20... | collective-permute-start | bytes 393224 | tf_op jit(solution)/shard_map/ppermute | solution.py:22
  18.9 4.3 %collective-permute-start.7 = (f32[4,32,128]{2,1,0:T(8,128)S(1)}, f32[4,32,128]{2,1,0:T(8,128)S(1)}, u32[]{:S(2)}, u32[]{:S(2)}) collective-permute-start(f32[4,32,128]{2,1,0:T(8,128)S(1)} %get-tuple-element.38), channel_id=1, source_target_pairs={{0,2},{2,0},{1,3},{3,1},{4,6},{6,4},{5,7},{7,5},{8,10},{10,8},{9,1... | collective-permute-start | bytes 196616 | tf_op jit(solution)/shard_map/ppermute | solution.py:22
  24.4 7.8 %collective-permute-start.8 = (f32[32,64,128]{2,1,0:T(8,128)S(1)}, f32[32,64,128]{2,1,0:T(8,128)S(1)}, u32[]{:S(2)}, u32[]{:S(2)}) collective-permute-start(f32[32,64,128]{2,1,0:T(8,128)S(1)} %get-tuple-element.40), channel_id=1, source_target_pairs={{0,16},{16,0},{1,17},{17,1},{2,18},{18,2},{3,19},{19,3},{4,20},{20... | collective-permute-start | bytes 3145736 | tf_op jit(solution)/shard_map/ppermute | solution.py:22
  24.4 7.7 %collective-permute-start.9 = (f32[4,64,128]{2,1,0:T(8,128)S(1)}, f32[4,64,128]{2,1,0:T(8,128)S(1)}, u32[]{:S(2)}, u32[]{:S(2)}) collective-permute-start(f32[4,64,128]{2,1,0:T(8,128)S(1)} %get-tuple-element.41), channel_id=1, source_target_pairs={{0,4},{8,12},{4,0},{12,8},{1,5},{9,13},{5,1},{13,9},{2,6},{10,14},... | collective-permute-start | bytes 393224 | tf_op jit(solution)/shard_map/ppermute | solution.py:22
  27.2 5.0 %collective-permute-start.10 = (f32[4,64,128]{2,1,0:T(8,128)S(1)}, f32[4,64,128]{2,1,0:T(8,128)S(1)}, u32[]{:S(2)}, u32[]{:S(2)}) collective-permute-start(f32[4,64,128]{2,1,0:T(8,128)S(1)} %get-tuple-element.42), channel_id=1, source_target_pairs={{4,8},{8,4},{5,9},{9,5},{6,10},{10,6},{7,11},{11,7},{20,24},{24,20... | collective-permute-start | bytes 393224 | tf_op jit(solution)/shard_map/ppermute | solution.py:22
  27.8 4.3 %collective-permute-start.11 = (f32[4,32,128]{2,1,0:T(8,128)S(1)}, f32[4,32,128]{2,1,0:T(8,128)S(1)}, u32[]{:S(2)}, u32[]{:S(2)}) collective-permute-start(f32[4,32,128]{2,1,0:T(8,128)S(1)} %get-tuple-element.43), channel_id=1, source_target_pairs={{0,2},{2,0},{1,3},{3,1},{4,6},{6,4},{5,7},{7,5},{8,10},{10,8},{9,1... | collective-permute-start | bytes 196616 | tf_op jit(solution)/shard_map/ppermute | solution.py:22
